TPU v7x, 64 devices: a 2x2x8 block of a 4x4x8 slice. The times are simulated.
64 devices in a mesh: rep: 8 (over x, y, core), dp: 8 (over z).
Axes of the slice: x: 2, y: 2, z: 8, core: 2. Of those that a mesh axis runs over, the one named last changes fastest.
The devices are a block of a 4x4x8 slice.
Arguments:
- x: bfloat16 [64, 2048, 640], P(('rep', 'dp')), parts along dimension 0
- dy: bfloat16 [64, 2048, 640], P(('rep', 'dp')), parts along dimension 0
- w_gate: bfloat16 [2, 640, 2176], replicated
- w_up: bfloat16 [2, 640, 2176], replicated
- w_down: bfloat16 [2, 2176, 640], replicated
- m_w_gate: float32 [2, 640, 2176], replicated
- m_w_up: float32 [2, 640, 2176], replicated
- m_w_down: float32 [2, 2176, 640], replicated
- v_w_gate: float32 [2, 640, 2176], replicated
- v_w_up: float32 [2, 640, 2176], replicated
- v_w_down: float32 [2, 2176, 640], replicated
Outputs:
- output 1: bfloat16 [16, 640, 2176], P('rep'), parts along dimension 0
- output 2: bfloat16 [16, 640, 2176], P('rep'), parts along dimension 0
- output 3: bfloat16 [16, 2176, 640], P('rep'), parts along dimension 0
- output 4: float32 [16, 640, 2176], P('rep'), parts along dimension 0
- output 5: float32 [16, 640, 2176], P('rep'), parts along dimension 0
- output 6: float32 [16, 2176, 640], P('rep'), parts along dimension 0
- output 7: float32 [16, 640, 2176], P('rep'), parts along dimension 0
- output 8: float32 [16, 640, 2176], P('rep'), parts along dimension 0
- output 9: float32 [16, 2176, 640], P('rep'), parts along dimension 0
There are 8 independent parts. A program takes and returns all parts, laid end to end along the dimension named above; an argument that names none is the same for every part.
All inputs are finite; a program needn't handle non-finite values.
Results may differ from a plain program's by a relative error of at most 0.022.
Values are sent between devices in bfloat16 or wider.
A program may use at most 768 MiB of HBM per device.

v0:
```python
import functools

import jax
import jax.numpy as jnp
from jax import lax
from jax.experimental import pallas as pl
from jax.experimental.pallas import tpu as pltpu
from jax.sharding import PartitionSpec as P


LANES = 128
FB = 2 * LANES
K1_ROWS = 512
S1_ROWS = 256
DA_ROWS = 512
STAGGER = 2
LEAD = 2
SLOTS = 12
S1_PARTS = 1
POINTS = S1_PARTS + 1
ALONE = 4
PACE = ((15, 10), (3, 2), (4, 3))
MIB = 1 << 20
MESH = pl.DeviceIdType.MESH
ANY = pl.BlockSpec(memory_space=pl.ANY)
bf16, f32 = jnp.bfloat16, jnp.float32


def wide(x):
    return x.astype(f32)


def dot(a, b, dims=((1,), (0,))):
    return lax.dot_general(a, b, (dims, ((), ())), preferred_element_type=f32)


def normed(h):
    h = wide(h)
    return (h * lax.rsqrt(jnp.mean(h * h, -1, keepdims=True) + 1e-6)).astype(bf16)


def adamw(w, m, v, g):
    m = 0.9 * m + 0.1 * g
    v = 0.95 * v + 0.05 * g * g
    step = m * lax.rsqrt(v + 1e-8) + 0.1 * w
    return (w - 0.02 * step).astype(bf16), m, v


def forward_kernel(h_ref, wg_ref, wu_ref, wd_ref, h1_ref, a1_ref, a1t_ref, a0_ref, a0t_ref, act_ref):
    ff = wg_ref.shape[-1]
    a = normed(h_ref[...])
    a0_ref[...] = a
    a0t_ref[...] = a.T
    for f in range(0, ff, FB):
        cols = slice(f, min(f + FB, ff))
        gate, up = dot(a, wg_ref[:, cols]), dot(a, wu_ref[:, cols])
        act_ref[:, cols] = (gate * jax.nn.sigmoid(gate) * up).astype(bf16)
    h1 = h_ref[...] + dot(act_ref[...], wd_ref[...]).astype(bf16)
    h1_ref[...] = h1
    a1 = normed(h1)
    a1_ref[...] = a1
    a1t_ref[...] = a1.T


def forward(x, wg, wu, wd):
    (tokens, d), ff = x.shape, wg.shape[-1]
    rows = pl.BlockSpec((K1_ROWS, d), lambda i: (i, 0))
    cols = pl.BlockSpec((d, K1_ROWS), lambda i: (0, i))
    once = functools.partial(pl.BlockSpec, index_map=lambda i: (0, 0, 0), pipeline_mode=pl.Buffered(1))
    up, across = jax.ShapeDtypeStruct((tokens, d), bf16), jax.ShapeDtypeStruct((d, tokens), bf16)
    return pl.pallas_call(
        forward_kernel,
        out_shape=(up, up, across, up, across),
        grid=(tokens // K1_ROWS,),
        in_specs=[rows, once((None, d, ff)), once((None, d, ff)), once((None, ff, d))],
        out_specs=(rows, rows, cols, rows, cols),
        scratch_shapes=[pltpu.VMEM((K1_ROWS, ff), bf16)],
        compiler_params=pltpu.CompilerParams(vmem_limit_bytes=56 * MIB),
        cost_estimate=pl.CostEstimate(flops=6 * tokens * d * ff, bytes_accessed=8 * d * ff, transcendentals=0),
        name="forward0",
    )(x, wg, wu, wd)


def backward_kernel(n, *refs):
    (a1, a1t, dy, h1, a0, a0t, wg, wu, wd, *out_refs), refs = refs[:11], refs[11:]
    (av, atv, dv, dgv, duv, actv, wgr, wur, wdr, wgf, wuf, hv, g_ref, ra, rb) = refs[:15]
    (sem_w, sem_in, sem_full, sem_h, sem_sa, sem_ra, sem_sb, sem_rb, free_a, free_b, sem_out) = refs[15:]
    tokens, d = av.shape
    ff = wg.shape[-1]
    units, lanes = g_ref.shape[:2]
    half = lanes // 2
    full = ff // FB
    blocks = full + 1
    rows = d // n
    rounds = n // 2

    me = lax.axis_index("dp")
    right, left = lax.rem(me + 1, n), lax.rem(me + n - 1, n)

    def shard(s):
        return pl.ds(pl.multiple_of(lax.rem(s, n) * rows, 16), rows)

    total = (units + STAGGER * (rounds - 1)) * rounds

    def turn(q):
        return rounds - 1 - lax.rem(q, rounds)

    def unit(q):
        return q // rounds - STAGGER * turn(q)

    def valid(q):
        return jnp.logical_and(q >= 0, jnp.logical_and(unit(q) >= 0, unit(q) < units))

    def copies(q, both):
        u, r, s = unit(q), turn(q), lax.rem(q, SLOTS)
        ca, cb = (pl.ds(0, lanes),) * 2 if both else (pl.ds(0, half), pl.ds(half, half))
        return (
            pltpu.make_async_remote_copy(
                g_ref.at[u, ca, shard(me + rounds - r)], ra.at[s, ca], sem_sa.at[s], sem_ra.at[s],
                device_id={"dp": right}, device_id_type=MESH,
            ),
            pltpu.make_async_remote_copy(
                g_ref.at[u, cb, shard(me + n - rounds + r)], rb.at[s, cb], sem_sb.at[s], sem_rb.at[s],
                device_id={"dp": left}, device_id_type=MESH,
            ),
        )

    def each(q, what):
        r = turn(q)

        @pl.when(r == 0)
        def _():
            for copy in copies(q, False):
                what(copy)

        @pl.when(r > 0)
        def _():
            for copy in copies(q, True):
                what(copy)

    def send(q):
        @pl.when(valid(q))
        def _():
            @pl.when(valid(q - SLOTS))
            def _():
                pl.semaphore_wait(free_a.at[lax.rem(q, SLOTS)], 1)
                pl.semaphore_wait(free_b.at[lax.rem(q, SLOTS)], 1)
                each(q - SLOTS, lambda c: c.wait_send())

            each(q, lambda c: c.start())

    def own(u, what):
        def to(out, k):
            what(pltpu.make_async_copy(g_ref.at[u, :, shard(me)], out.at[k], sem_out.at[u]))

        @pl.when(u < full)
        def _():
            to(out_refs[0], u)

        @pl.when(u == units - 1)
        def _():
            to(out_refs[0], full)

        @pl.when(jnp.logical_and(u >= full, u < units - 1))
        def _():
            to(out_refs[1], u - full)

    def start(u):
        send(u * rounds + rounds - 1)

    def serve(q, ready):
        @pl.when(valid(q))
        def _():
            u, r, s = unit(q), turn(q), lax.rem(q, SLOTS)
            at, bt = shard(me + rounds - 1 - r), shard(me + n - rounds + 1 + r)
            each(q, lambda c: c.wait_recv())

            @pl.when(r == 0)
            def _():
                g_ref[u, :half, at] = (wide(g_ref[u, :half, at]) + wide(ra[s, :half])).astype(bf16)
                g_ref[u, half:, bt] = (wide(g_ref[u, half:, bt]) + wide(rb[s, half:])).astype(bf16)

            @pl.when(jnp.logical_and(r > 0, r < rounds - 1))
            def _():
                g_ref[u, :, at] = (wide(g_ref[u, :, at]) + wide(ra[s])).astype(bf16)
                g_ref[u, :, bt] = (wide(g_ref[u, :, bt]) + wide(rb[s])).astype(bf16)

            @pl.when(r == rounds - 1)
            def _():
                g_ref[u, :, at] = (wide(g_ref[u, :, at]) + wide(ra[s]) + wide(rb[s])).astype(bf16)

            @pl.when(valid(q + SLOTS))
            def _():
                pl.semaphore_signal(free_a.at[s], inc=1, device_id={"dp": left}, device_id_type=MESH)
                pl.semaphore_signal(free_b.at[s], inc=1, device_id={"dp": right}, device_id_type=MESH)

            @pl.when(r == rounds - 1)
            def _():
                own(u, lambda c: c.start())

            @pl.when(r < rounds - 1)
            def _():
                send(q + STAGGER * rounds - 1)

            @pl.when(jnp.logical_and(r == 0, u + LEAD < ready))
            def _():
                start(u + LEAD)

    def serve_all(first, last, ready):
        def one(q, carry):
            serve(q, ready)
            return carry

        lax.fori_loop(first, last, one, 0)

    def paced(pace, k):
        return k * pace[0] // pace[1]

    first = (ALONE - 1) * rounds + paced(PACE[0], POINTS * (blocks - ALONE))
    later = first + paced(PACE[1], tokens // DA_ROWS)
    finish = later + paced(PACE[2], POINTS * blocks)

    def served(b, i):
        regular = jnp.where(
            b < blocks,
            (ALONE - 1) * rounds + paced(PACE[0], POINTS * (b - ALONE) + i + 1),
            later + paced(PACE[2], POINTS * (b - blocks) + i + 1),
        )
        alone = jnp.maximum(b - 1 + (i == POINTS - 1), 0) * rounds
        return jnp.where(b < ALONE, alone, regular)

    def ready(b):
        return jnp.where(b < blocks, jnp.minimum(b, full), b - 1)

    def point(b, i):
        if i < POINTS - 1:
            serve_all(served(b, i - 1), served(b, i), ready(b))
            return
        made = ready(b + 1)
        u = made - 1

        @pl.when(jnp.logical_and(made > ready(b), jnp.logical_or(u < LEAD, served(b, i - 1) >= (u - LEAD + 1) * rounds)))
        def _():
            start(u)

        serve_all(served(b, i - 1), served(b, i), made)

    loads = [
        pltpu.make_async_copy(src, dst, sem_in.at[i])
        for i, (src, dst) in enumerate(((a1, av), (dy, dv), (a1t, atv)))
    ]
    second = [pltpu.make_async_copy(src, dst, sem_in.at[i]) for i, (src, dst) in enumerate(((a0, av), (a0t, atv)))]
    whole = [pltpu.make_async_copy(src.at[1], dst, sem_full.at[i]) for i, (src, dst) in enumerate(((wg, wgf), (wu, wuf)))]

    def place(b):
        layer = jnp.where(b < blocks, 1, 0)
        j = jnp.where(b < blocks, b, b - blocks)
        return layer, j, pl.multiple_of(jnp.minimum(j * FB, ff - FB), LANES)

    def weights(b):
        layer, _, c = place(b)
        s = lax.rem(b, 2)
        return (
            pltpu.make_async_copy(wg.at[layer, :, pl.ds(c, FB)], wgr.at[s], sem_w.at[0, s]),
            pltpu.make_async_copy(wu.at[layer, :, pl.ds(c, FB)], wur.at[s], sem_w.at[1, s]),
            pltpu.make_async_copy(wd.at[layer, pl.ds(c, FB), :], wdr.at[s], sem_w.at[2, s]),
        )

    for copy in (*weights(jnp.int32(0)), *loads[:2]):
        copy.start()
    barrier = pltpu.get_barrier_semaphore()
    for neighbour in (left, right):
        pl.semaphore_signal(barrier, inc=1, device_id={"dp": neighbour}, device_id_type=MESH)
    for copy in loads[2:]:
        copy.start()
    for copy in loads[:2]:
        copy.wait()
    pl.semaphore_wait(barrier, 2)

    def h_tile(t):
        return pltpu.make_async_copy(h1.at[pl.ds(t * DA_ROWS, DA_ROWS)], hv.at[lax.rem(t, 2)], sem_h.at[lax.rem(t, 2)])

    def through_norm():
        da_tiles = tokens // DA_ROWS
        for copy in second:
            copy.start()
        for copy in whole:
            copy.wait()
        h_tile(jnp.int32(0)).start()

        def tile(t, carry):
            r = pl.ds(pl.multiple_of(t * DA_ROWS, DA_ROWS), DA_ROWS)

            @pl.when(t + 1 < da_tiles)
            def _():
                h_tile(t + 1).start()

            h_tile(t).wait()
            last = ((1,), (1,))
            da = wide(dot(dgv[r, :], wgf[...], last).astype(bf16)) + wide(dot(duv[r, :], wuf[...], last).astype(bf16))
            da = wide(da.astype(bf16))
            h = wide(hv[lax.rem(t, 2)])
            scale = lax.rsqrt(jnp.mean(h * h, -1, keepdims=True) + 1e-6)
            dh = (da * scale - h * (scale * scale * scale * jnp.mean(da * h, -1, keepdims=True))).astype(bf16)
            dh = (wide(dv[r, :]) + wide(dh)).astype(bf16)
            dv[r, :] = dh
            serve_all(first + paced(PACE[1], t), first + paced(PACE[1], t + 1), full)
            return carry

        lax.fori_loop(0, da_tiles, tile, 0)
        for copy in second:
            copy.wait()

    def block(b, carry):
        layer, j, c = place(b)
        s = lax.rem(b, 2)
        cols = pl.ds(c, FB)
        for copy in weights(b):
            copy.wait()

        @pl.when(b + 1 < 2 * blocks)
        def _():
            for copy in weights(b + 1):
                copy.start()

        @pl.when(b == 1)
        def _():
            for copy in whole:
                copy.start()

        @pl.when(b == blocks)
        def _():
            through_norm()

        def products(r):
            return dot(av[r, :], wgr[s]), dot(av[r, :], wur[s]), dot(dv[r, :], wdr[s], ((1,), (1,)))

        def pointwise(r, gate, up, dact):
            dact = wide(dact.astype(bf16))
            sig = jax.nn.sigmoid(gate)
            silu = gate * sig
            actv[r, :] = (silu * up).astype(bf16)
            duv[r, cols] = (dact * silu).astype(bf16)
            dgv[r, cols] = (dact * up * (sig + silu * (1.0 - sig))).astype(bf16)

        for i in range(S1_PARTS):
            before = None
            for t in range(tokens // S1_ROWS // S1_PARTS * i, tokens // S1_ROWS // S1_PARTS * (i + 1)):
                r = slice(t * S1_ROWS, (t + 1) * S1_ROWS)
                made = products(r)
                if before is not None:
                    pointwise(*before)
                before = (r, *made)
            pointwise(*before)
            point(b, i)

        @pl.when(b == 0)
        def _():
            for copy in loads[2:]:
                copy.wait()

        rest = j == full
        u = jnp.where(rest, units - 1, jnp.where(layer == 1, j, full + j))
        h0, h1_ = jnp.where(rest, 1 - layer, 0), jnp.where(rest, 1 - layer, 1)
        dwg = dot(atv[...], dgv[:, cols]).astype(bf16)
        dwu = dot(atv[...], duv[:, cols]).astype(bf16)
        dwd = dot(actv[...], dv[...], ((0,), (0,))).astype(bf16)
        for h, k in ((h0, 0), (h1_, LANES)):
            g_ref[u, h] = dwg[:, k : k + LANES]
            g_ref[u, half + h] = dwu[:, k : k + LANES]
            g_ref[u, half - 1 + half * h] = jnp.concatenate(
                [
                    dwd[k + LANES // n * s_ : k + LANES // n * (s_ + 1), c_ : c_ + LANES]
                    for s_ in range(n)
                    for c_ in range(0, d, LANES)
                ],
                0,
            )
        point(b, POINTS - 1)
        return carry

    lax.fori_loop(0, 2 * blocks, block, 0)
    serve_all(finish, total, units)

    def sent(q, carry):
        @pl.when(jnp.logical_and(valid(q), jnp.logical_not(valid(q + SLOTS))))
        def _():
            each(q, lambda c: c.wait_send())

        return carry

    lax.fori_loop(0, total, sent, 0)

    def written(u, carry):
        own(u, lambda c: c.wait())
        return carry

    lax.fori_loop(0, units, written, 0)


def backward(n, a1, a1t, dy, h1, a0, a0t, wg, wu, wd):
    (tokens, d), (layers, _, ff) = a1.shape, wg.shape
    full, lanes = ff // FB, 3 * FB // LANES
    units = layers * full + 1
    assert layers == 2 and ff % FB == LANES and d % (16 * n) == 0 and LANES // n * (d // LANES) == d // n
    assert SLOTS % (n // 2) == 0 and LEAD + 1 <= SLOTS // (n // 2)
    dma, vmem = pltpu.SemaphoreType.DMA, lambda *shape: pltpu.VMEM(shape, bf16)
    return pl.pallas_call(
        functools.partial(backward_kernel, n),
        out_shape=tuple(jax.ShapeDtypeStruct((size, lanes, d // n, LANES), bf16) for size in (full + 1, full)),
        in_specs=[ANY] * 9,
        out_specs=(ANY,) * 2,
        scratch_shapes=[
            vmem(tokens, d), vmem(d, tokens), vmem(tokens, d), vmem(tokens, ff), vmem(tokens, ff),
            vmem(tokens, FB), vmem(2, d, FB), vmem(2, d, FB), vmem(2, FB, d), vmem(d, ff), vmem(d, ff),
            vmem(2, DA_ROWS, d), vmem(units, lanes, d, LANES),
            vmem(SLOTS, lanes, d // n, LANES), vmem(SLOTS, lanes, d // n, LANES),
            dma((3, 2)), dma((3,)), dma((2,)), dma((2,)), dma((SLOTS,)), dma((SLOTS,)), dma((SLOTS,)), dma((SLOTS,)),
            pltpu.SemaphoreType.REGULAR((SLOTS,)), pltpu.SemaphoreType.REGULAR((SLOTS,)), dma((units,)),
        ],
        compiler_params=pltpu.CompilerParams(collective_id=0, has_side_effects=True, vmem_limit_bytes=67043328),
        cost_estimate=pl.CostEstimate(flops=24 * tokens * d * ff, bytes_accessed=40 * d * ff, transcendentals=0),
        name="backward_reduce",
    )(a1, a1t, dy, h1, a0, a0t, wg, wu, wd)


def gather(n, mine):
    right, left = [(i, (i + 1) % n) for i in range(n)], [(i, (i - 1) % n) for i in range(n)]

    def both(to_right, to_left):
        from_left = lax.ppermute(to_right, "dp", right)
        return from_left, lax.ppermute(to_left, "dp", left)

    from_left = from_right = mine
    rounds = [[(0, mine)]]
    for r in range(1, n // 2):
        from_left, from_right = both(from_left, from_right)
        rounds.append([(n - r, from_left), (r, from_right)])
    half = mine.shape[1] // 2
    return [*rounds, [(n // 2, both(from_left[:, :half], from_right[:, half:]))]]


def adamw_kernel(entries, paired, side, counts, aliased, ids_ref, *refs):
    per = 2 if paired else 1
    grads, refs = refs[: entries * per * len(counts)], refs[entries * per * len(counts) :]
    ins, outs = refs[:9], refs[9 + 9 * aliased :]
    w, m, v = ins[:3], ins[3:6], ins[6:]
    fine, steps = w[2].shape[1], w[2].shape[2] // LANES
    lanes = grads[0].shape[1] * per
    half = lanes // 2
    full = counts[0] - (len(counts) == 1)
    places = [(0, unit, h) for unit in range(full) for h in range(2)]
    places.append((len(counts) - 1, full if len(counts) == 1 else 0, side))

    def step(e):
        def part(j, carry):
            rows = pl.ds(pl.multiple_of(j * fine, fine), fine)
            tile = pl.ds(pl.multiple_of(j * LANES, LANES), LANES)

            def lane(source, unit, k):
                refs = grads[(source * entries + e) * per : (source * entries + e + 1) * per]
                return wide(refs[k // half][unit, k % half, rows] if paired else refs[0][unit, k, rows])

            for at, (source, unit, h) in enumerate(places):
                cols = slice(at * LANES, (at + 1) * LANES)
                for i, where, k in ((0, (rows, cols), h), (1, (rows, cols), half + h), (2, (at, slice(None), tile), half - 1 + half * h)):
                    new = adamw(wide(w[i][where]), m[i][where], v[i][where], lane(source, unit, k))
                    for out, value in zip(outs[i::3], new, strict=True):
                        out[where] = value
            return carry

        lax.fori_loop(0, steps, part, 0)

    for e in range(entries):
        pl.when(pl.program_id(0) == e)(functools.partial(step, e))


def optimizer(n, layer, me, shards, mixed, arrays, before):
    paired = isinstance(shards[0][1], tuple)
    flat = lambda many: [a for _, b in many for a in (b if paired else (b,))]
    grads = flat(shards) + (flat(mixed) if mixed else [])
    rows = grads[0].shape[2]
    _, d, ff = arrays[0].shape
    steps = d // LANES
    assert rows % steps == 0 and rows // steps == LANES // n
    fine = rows // steps
    ids = jnp.concatenate([lax.rem(me + o, n) for o, _ in shards])

    def block(array, whole):
        units = array.shape[0]
        if whole:
            return pl.BlockSpec(array.shape, lambda i, _: (0, 0, 0, 0), pipeline_mode=pl.Buffered(1))
        return pl.BlockSpec((1, *array.shape[1:]), lambda i, _: (units - 1, 0, 0, 0), pipeline_mode=pl.Buffered(1))

    per = 2 if paired else 1
    specs = [block(a, k < len(shards) * per) for k, a in enumerate(grads)]
    up = pl.BlockSpec((None, rows, ff), lambda i, ids: (layer, ids[i], 0))
    down = pl.BlockSpec((None, ff // LANES, fine, d), lambda i, ids: (layer, 0, ids[i], 0))
    spec = [up, up, down] * 3
    counts = [shards[0][1][0].shape[0] if paired else shards[0][1].shape[0]] + ([1] if mixed else [])
    old = () if before is None else before
    return pl.pallas_call(
        functools.partial(adamw_kernel, len(shards), paired, 1 - layer, counts, bool(old)),
        out_shape=tuple(jax.ShapeDtypeStruct(a.shape, a.dtype) for a in arrays),
        grid_spec=pltpu.PrefetchScalarGridSpec(
            num_scalar_prefetch=1, grid=(len(shards),), in_specs=specs + spec + [ANY] * len(old), out_specs=tuple(spec)
        ),
        input_output_aliases={1 + len(grads) + 9 + i: i for i in range(len(old))},
        compiler_params=pltpu.CompilerParams(vmem_limit_bytes=60 * MIB),
        cost_estimate=pl.CostEstimate(
            flops=len(shards) * rows * ff * 3 * 4000, bytes_accessed=len(shards) * rows * ff * 3 * 22, transcendentals=0
        ),
        name="adamw",
    )(ids, *grads, *arrays, *old)


def solution(mesh):
    n = mesh.shape["dp"]

    def step(x, dy, *arrays):
        wg, wu, wd = arrays[:3]
        x, dy = x[0], dy[0]
        h1, a1, a1t, a0, a0t = forward(x, wg, wu, wd)
        second, first = backward(n, a1, a1t, dy, h1, a0, a0t, wg, wu, wd)
        me = lax.axis_index("dp").astype(jnp.int32)[None]
        shapes = [a.shape for a in arrays]
        arrays = [a.reshape(a.shape[0], -1, LANES, a.shape[2]) if i % 3 == 2 else a for i, a in enumerate(arrays)]
        new = None
        for of_second, of_first in zip(gather(n, second), gather(n, first), strict=True):
            new = optimizer(n, 1, me, of_second, None, arrays, new)
            new = optimizer(n, 0, me, of_first, of_second, arrays, new)
        return tuple(a.reshape(shape) for a, shape in zip(new, shapes, strict=True))

    return jax.shard_map(
        step,
        mesh=mesh,
        in_specs=(P(("rep", "dp"), None, None),) * 2 + (P(None, None, None),) * 9,
        out_specs=(P("rep", None, None),) * 9,
        check_vma=False,
    )
```

profile of v0, /device:TPU:21, one launch (start us, length us, event | category | flops | bytes accessed | tf_op | source)
XLA Modules:
  0.0 391.3 jit_solution(1088127296330072743)
XLA Ops:
  0.6 29.0 %forward0.1 = (bf16[2048,640]{1,0:T(8,128)(2,1)}, bf16[2048,640]{1,0:T(8,128)(2,1)}, bf16[640,2048]{1,0:T(8,128)(2,1)}, bf16[2048,640]{1,0:T(8,128)(2,1)}, bf16[640,2048]{1,0:T(8,128)(2,1)}) custom-call(bf16[2048,640]{1,0:T(8,128)(2,1)} %bitcast.42, bf16[2,640,2176]{2,1,0:T(8,128)(2,1)} %refs_4_.9, bf16[2,640,2176]{2,1,0:T(8,128)(2,1)} %refs_5_.19, ...), custom_call_target="tpu_custom_call" | custom-call | flops 17112760320 | bytes 11141120 | tf_op jit(solution)/shard_map/forward0/pallas_call | solution.py:71
  29.6 187.7 %backward_reduce.1 = (bf16[9,6,80,128]{3,2,1,0:T(8,128)(2,1)}, bf16[8,6,80,128]{3,2,1,0:T(8,128)(2,1)}) custom-call(bf16[2048,640]{1,0:T(8,128)(2,1)} %get-tuple-element.106.refs_0_, bf16[640,2048]{1,0:T(8,128)(2,1)} %get-tuple-element.107.refs_1_, bf16[2048,640]{1,0:T(8,128)(2,1)} %bitcast.43, bf16[2048,640]{1,0:T(8,128)(2,1)} %get-tuple-element.108.refs_3_, ...), custom_call_target="tpu_custom_call" | custom-call | flops 68451041280 | bytes 55705600 | tf_op jit(solution)/shard_map/backward_reduce/pallas_call | solution.py:408
  217.3 1.5 collective-permute-start.12
  218.8 0.1 collective-permute-start.8
  218.9 0.4 collective-permute-start
  219.3 2.2 collective-permute-start.4
  221.6 19.5 %collective-permute-done.12.refs_1_.refs_3_ = bf16[9,6,80,128]{3,2,1,0:T(8,128)(2,1)S(1)} collective-permute-done((bf16[9,6,80,128]{3,2,1,0:T(8,128)(2,1)}, bf16[9,6,80,128]{3,2,1,0:T(8,128)(2,1)S(1)}, u32[]{:S(2)}, u32[]{:S(2)}) %collective-permute-start.12) | collective-permute-done | bytes 1105952 | tf_op jit(solution)/shard_map/ppermute | solution.py:432
  241.0 0.0 copy-start.2
  241.0 3.1 collective-permute-start.13
  244.1 0.0 collective-permute-done.8.refs_0_.refs_2_
  244.1 0.0 copy-start.3
  244.1 0.0 collective-permute-start.9
  244.1 0.6 pad_add_fusion.2.ids_ref
  244.8 20.2 %collective-permute-done.refs_0_ = bf16[8,6,80,128]{3,2,1,0:T(8,128)(2,1)} collective-permute-done((bf16[8,6,80,128]{3,2,1,0:T(8,128)(2,1)}, bf16[8,6,80,128]{3,2,1,0:T(8,128)(2,1)}, u32[]{:S(2)}, u32[]{:S(2)}) %collective-permute-start) | collective-permute-done | bytes 983072 | tf_op jit(solution)/shard_map/ppermute | solution.py:431
  265.0 0.0 collective-permute-start.1
  265.0 0.0 collective-permute-done.4.refs_1_
  265.0 2.7 collective-permute-start.5
  267.7 0.6 pad_add_fusion.1.ids_ref
  268.4 0.6 pad_add_fusion.ids_ref
  269.0 6.4 %adamw.10 = (bf16[2,640,2176]{2,1,0:T(8,128)(2,1)}, bf16[2,640,2176]{2,1,0:T(8,128)(2,1)}, bf16[2,17,128,640]{3,2,1,0:T(8,128)(2,1)}, f32[2,640,2176]{2,1,0:T(8,...) custom-call(s32[1]{0:T(128)S(6)} %rem.159.ids_ref, ...), custom_call_target="tpu_custom_call" | custom-call | flops 2088960000 | bytes 11489280 | tf_op jit(solution)/shard_map/adamw/pallas_call | solution.py:502
  275.3 0.0 copy-done.2
  275.3 0.0 copy-done.3
  275.3 6.5 %adamw.11 = (bf16[2,640,2176]{2,1,0:T(8,128)(2,1)}, bf16[2,640,2176]{2,1,0:T(8,128)(2,1)}, bf16[2,17,128,640]{3,2,1,0:T(8,128)(2,1)}, f32[2,640,2176]{2,1,0:T(8,...) custom-call(s32[1]{0:T(128)S(6)} %rem.159.ids_ref, ...), custom_call_target="tpu_custom_call", output_to_operand_aliasing={{0}: (12, {}), {1}: (13, {}), {2}: (14, {}), {3}: (15, {}),... | custom-call | flops 2088960000 | bytes 11489280 | tf_op jit(solution)/shard_map/adamw/pallas_call | solution.py:502
  281.8 9.2 %adamw.12 = (bf16[2,640,2176]{2,1,0:T(8,128)(2,1)}, bf16[2,640,2176]{2,1,0:T(8,128)(2,1)}, bf16[2,17,128,640]{3,2,1,0:T(8,128)(2,1)}, f32[2,640,2176]{2,1,0:T(8,...) custom-call(s32[2]{0:T(128)} %pad_add_fusion.2.ids_ref, ...), custom_call_target="tpu_custom_call", output_to_operand_aliasing={{0}: (12, {}), {1}: (13, {}), {2}: (14, {}), {3}: (15, {}),... | custom-call | flops 4177920000 | bytes 22978560 | tf_op jit(solution)/shard_map/adamw/pallas_call | solution.py:502
  291.0 18.8 %collective-permute-done.1.refs_0_ = bf16[8,6,80,128]{3,2,1,0:T(8,128)(2,1)} collective-permute-done((bf16[8,6,80,128]{3,2,1,0:T(8,128)(2,1)}, bf16[8,6,80,128]{3,2,1,0:T(8,128)(2,1)}, u32[]{:S(2)}, u32[]{:S(2)}) %collective-permute-start.1) | collective-permute-done | bytes 983072 | tf_op jit(solution)/shard_map/ppermute | solution.py:431
  309.8 0.0 collective-permute-start.2
  309.8 0.0 collective-permute-done.5.refs_1_
  309.8 2.7 collective-permute-start.6
  312.5 0.0 collective-permute-done.9.refs_0_.refs_2_
  312.5 0.0 collective-permute-start.10
  312.5 0.0 collective-permute-done.13.refs_1_.refs_3_
  312.5 2.7 collective-permute-start.14
  315.2 9.1 %adamw.13 = (bf16[2,640,2176]{2,1,0:T(8,128)(2,1)}, bf16[2,640,2176]{2,1,0:T(8,128)(2,1)}, bf16[2,17,128,640]{3,2,1,0:T(8,128)(2,1)}, f32[2,640,2176]{2,1,0:T(8,...) custom-call(s32[2]{0:T(128)} %pad_add_fusion.2.ids_ref, ...), custom_call_target="tpu_custom_call", output_to_operand_aliasing={{0}: (14, {}), {1}: (15, {}), {2}: (16, {}), {3}: (17, {}),... | custom-call | flops 4177920000 | bytes 22978560 | tf_op jit(solution)/shard_map/adamw/pallas_call | solution.py:502
  324.3 9.3 %adamw.14 = (bf16[2,640,2176]{2,1,0:T(8,128)(2,1)}, bf16[2,640,2176]{2,1,0:T(8,128)(2,1)}, bf16[2,17,128,640]{3,2,1,0:T(8,128)(2,1)}, f32[2,640,2176]{2,1,0:T(8,...) custom-call(s32[2]{0:T(128)} %pad_add_fusion.1.ids_ref, ...), custom_call_target="tpu_custom_call", output_to_operand_aliasing={{0}: (12, {}), {1}: (13, {}), {2}: (14, {}), {3}: (15, {}),... | custom-call | flops 4177920000 | bytes 22978560 | tf_op jit(solution)/shard_map/adamw/pallas_call | solution.py:502
  333.6 9.2 %adamw.15 = (bf16[2,640,2176]{2,1,0:T(8,128)(2,1)}, bf16[2,640,2176]{2,1,0:T(8,128)(2,1)}, bf16[2,17,128,640]{3,2,1,0:T(8,128)(2,1)}, f32[2,640,2176]{2,1,0:T(8,...) custom-call(s32[2]{0:T(128)} %pad_add_fusion.1.ids_ref, ...), custom_call_target="tpu_custom_call", output_to_operand_aliasing={{0}: (14, {}), {1}: (15, {}), {2}: (16, {}), {3}: (17, {}),... | custom-call | flops 4177920000 | bytes 22978560 | tf_op jit(solution)/shard_map/adamw/pallas_call | solution.py:502
  342.8 0.0 collective-permute-done.2.refs_0_
  342.8 1.8 slice.16
  344.7 0.0 collective-permute-start.3
  344.7 0.0 collective-permute-done.6.refs_1_
  344.7 1.8 slice.17
  346.5 2.7 collective-permute-start.7
  349.2 5.9 %collective-permute-done.10.refs_0_.refs_2_ = bf16[9,6,80,128]{3,2,1,0:T(8,128)(2,1)S(1)} collective-permute-done((bf16[9,6,80,128]{3,2,1,0:T(8,128)(2,1)}, bf16[9,6,80,128]{3,2,1,0:T(8,128)(2,1)S(1)}, u32[]{:S(2)}, u32[]{:S(2)}) %collective-permute-start.10) | collective-permute-done | bytes 1105952 | tf_op jit(solution)/shard_map/ppermute | solution.py:431
  355.1 0.0 copy-start
  355.1 0.1 collective-permute-start.11
  355.2 0.0 collective-permute-done.14.refs_1_.refs_3_
  355.3 0.0 copy-start.1
  355.3 1.0 slice.19
  356.3 2.5 collective-permute-start.15
  358.8 0.0 copy-done
  358.8 0.0 copy-done.1
  358.8 9.2 %adamw.16 = (bf16[2,640,2176]{2,1,0:T(8,128)(2,1)}, bf16[2,640,2176]{2,1,0:T(8,128)(2,1)}, bf16[2,17,128,640]{3,2,1,0:T(8,128)(2,1)}, f32[2,640,2176]{2,1,0:T(8,...) custom-call(s32[2]{0:T(128)} %pad_add_fusion.ids_ref, ...), custom_call_target="tpu_custom_call", output_to_operand_aliasing={{0}: (12, {}), {1}: (13, {}), {2}: (14, {}), {3}: (15, {}),... | custom-call | flops 4177920000 | bytes 22978560 | tf_op jit(solution)/shard_map/adamw/pallas_call | solution.py:502
  368.0 9.2 %adamw.17 = (bf16[2,640,2176]{2,1,0:T(8,128)(2,1)}, bf16[2,640,2176]{2,1,0:T(8,128)(2,1)}, bf16[2,17,128,640]{3,2,1,0:T(8,128)(2,1)}, f32[2,640,2176]{2,1,0:T(8,...) custom-call(s32[2]{0:T(128)} %pad_add_fusion.ids_ref, ...), custom_call_target="tpu_custom_call", output_to_operand_aliasing={{0}: (14, {}), {1}: (15, {}), {2}: (16, {}), {3}: (17, {}),... | custom-call | flops 4177920000 | bytes 22978560 | tf_op jit(solution)/shard_map/adamw/pallas_call | solution.py:502
  377.3 0.2 collective-permute-done.11.refs_0_.refs_2_
  377.5 0.0 copy-start.4
  377.5 0.0 collective-permute-done.15.refs_1_.refs_3_
  377.5 0.0 copy-start.5
  377.5 0.8 copy-done.4
  378.3 0.2 copy-done.5
  378.5 6.4 %adamw.18 = (bf16[2,640,2176]{2,1,0:T(8,128)(2,1)}, bf16[2,640,2176]{2,1,0:T(8,128)(2,1)}, bf16[2,17,128,640]{3,2,1,0:T(8,128)(2,1)}, f32[2,640,2176]{2,1,0:T(8,...) custom-call(s32[1]{0:T(128)S(6)} %rem.117.ids_ref, ...), custom_call_target="tpu_custom_call", output_to_operand_aliasing={{0}: (12, {}), {1}: (13, {}), {2}: (14, {}), {3}: (15, {}),... | custom-call | flops 2088960000 | bytes 11489280 | tf_op jit(solution)/shard_map/adamw/pallas_call | solution.py:502
  384.8 0.0 collective-permute-done.3.refs_0_
  384.8 0.0 collective-permute-done.7.refs_1_
  384.8 6.4 %adamw.19 = (bf16[2,640,2176]{2,1,0:T(8,128)(2,1)}, bf16[2,640,2176]{2,1,0:T(8,128)(2,1)}, bf16[2,17,128,640]{3,2,1,0:T(8,128)(2,1)}, f32[2,640,2176]{2,1,0:T(8,...) custom-call(s32[1]{0:T(128)S(6)} %rem.117.ids_ref, ...), custom_call_target="tpu_custom_call", output_to_operand_aliasing={{0}: (14, {}), {1}: (15, {}), {2}: (16, {}), {3}: (17, {}),... | custom-call | flops 2088960000 | bytes 11489280 | tf_op jit(solution)/shard_map/adamw/pallas_call | solution.py:502
  (1 shorter events, 0.0 us)
Async XLA Ops:
  217.3 23.7 %collective-permute-start.12 = (bf16[9,6,80,128]{3,2,1,0:T(8,128)(2,1)}, bf16[9,6,80,128]{3,2,1,0:T(8,128)(2,1)S(1)}, u32[]{:S(2)}, u32[]{:S(2)}) collective-permute-start(bf16[9,6,80,128]{3,2,1,0:T(8,128)(2,1)} %get-tuple-element.112.refs_0_.refs_1_), channel_id=1, source_target_pairs={{0,7},{1,0},{2,1},{3,2},{4,3},{5,4},{6,5},{7,6},{8,15},{9,8},{10,9... | collective-permute-start | bytes 3317768 | tf_op jit(solution)/shard_map/ppermute | solution.py:432
  218.8 25.4 %collective-permute-start.8 = (bf16[9,6,80,128]{3,2,1,0:T(8,128)(2,1)}, bf16[9,6,80,128]{3,2,1,0:T(8,128)(2,1)S(1)}, u32[]{:S(2)}, u32[]{:S(2)}) collective-permute-start(bf16[9,6,80,128]{3,2,1,0:T(8,128)(2,1)} %get-tuple-element.112.refs_0_.refs_1_), channel_id=1, source_target_pairs={{0,1},{1,2},{2,3},{3,4},{4,5},{5,6},{6,7},{7,0},{8,9},{9,10},{10,1... | collective-permute-start | bytes 3317768 | tf_op jit(solution)/shard_map/ppermute | solution.py:431
  218.9 46.1 %collective-permute-start = (bf16[8,6,80,128]{3,2,1,0:T(8,128)(2,1)}, bf16[8,6,80,128]{3,2,1,0:T(8,128)(2,1)}, u32[]{:S(2)}, u32[]{:S(2)}) collective-permute-start(bf16[8,6,80,128]{3,2,1,0:T(8,128)(2,1)} %get-tuple-element.111.refs_0_), channel_id=1, source_target_pairs={{0,1},{1,2},{2,3},{3,4},{4,5},{5,6},{6,7},{7,0},{8,9},{9,10},{10,1... | collective-permute-start | bytes 2949128 | tf_op jit(solution)/shard_map/ppermute | solution.py:431
  219.3 45.7 %collective-permute-start.4 = (bf16[8,6,80,128]{3,2,1,0:T(8,128)(2,1)}, bf16[8,6,80,128]{3,2,1,0:T(8,128)(2,1)}, u32[]{:S(2)}, u32[]{:S(2)}) collective-permute-start(bf16[8,6,80,128]{3,2,1,0:T(8,128)(2,1)} %get-tuple-element.111.refs_0_), channel_id=1, source_target_pairs={{0,7},{1,0},{2,1},{3,2},{4,3},{5,4},{6,5},{7,6},{8,15},{9,8},{10,9... | collective-permute-start | bytes 2949128 | tf_op jit(solution)/shard_map/ppermute | solution.py:432
  241.0 34.3 %copy-start.2 = (bf16[9,6,80,128]{3,2,1,0:T(8,128)(2,1)}, bf16[9,6,80,128]{3,2,1,0:T(8,128)(2,1)S(1)}, u32[]{:S(2)}) copy-start(bf16[9,6,80,128]{3,2,1,0:T(8,128)(2,1)S(1)} %collective-permute-done.12.refs_1_.refs_3_) | copy-start | bytes 3317764
  241.0 71.5 %collective-permute-start.13 = (bf16[9,6,80,128]{3,2,1,0:T(8,128)(2,1)S(1)}, bf16[9,6,80,128]{3,2,1,0:T(8,128)(2,1)}, u32[]{:S(2)}, u32[]{:S(2)}) collective-permute-start(bf16[9,6,80,128]{3,2,1,0:T(8,128)(2,1)S(1)} %collective-permute-done.12.refs_1_.refs_3_), channel_id=1, source_target_pairs={{0,7},{1,0},{2,1},{3,2},{4,3},{5,4},{6,5},{7,6},{8,15},{9,8},{10,9... | collective-permute-start | bytes 3317768 | tf_op jit(solution)/shard_map/ppermute | solution.py:432
  244.1 31.2 %copy-start.3 = (bf16[9,6,80,128]{3,2,1,0:T(8,128)(2,1)}, bf16[9,6,80,128]{3,2,1,0:T(8,128)(2,1)S(1)}, u32[]{:S(2)}) copy-start(bf16[9,6,80,128]{3,2,1,0:T(8,128)(2,1)S(1)} %collective-permute-done.8.refs_0_.refs_2_) | copy-start | bytes 3317764
  244.1 68.3 %collective-permute-start.9 = (bf16[9,6,80,128]{3,2,1,0:T(8,128)(2,1)S(1)}, bf16[9,6,80,128]{3,2,1,0:T(8,128)(2,1)}, u32[]{:S(2)}, u32[]{:S(2)}) collective-permute-start(bf16[9,6,80,128]{3,2,1,0:T(8,128)(2,1)S(1)} %collective-permute-done.8.refs_0_.refs_2_), channel_id=1, source_target_pairs={{0,1},{1,2},{2,3},{3,4},{4,5},{5,6},{6,7},{7,0},{8,9},{9,10},{10,1... | collective-permute-start | bytes 3317768 | tf_op jit(solution)/shard_map/ppermute | solution.py:431
  265.0 44.8 %collective-permute-start.1 = (bf16[8,6,80,128]{3,2,1,0:T(8,128)(2,1)}, bf16[8,6,80,128]{3,2,1,0:T(8,128)(2,1)}, u32[]{:S(2)}, u32[]{:S(2)}) collective-permute-start(bf16[8,6,80,128]{3,2,1,0:T(8,128)(2,1)} %collective-permute-done.refs_0_), channel_id=1, source_target_pairs={{0,1},{1,2},{2,3},{3,4},{4,5},{5,6},{6,7},{7,0},{8,9},{9,10},{10,1... | collective-permute-start | bytes 2949128 | tf_op jit(solution)/shard_map/ppermute | solution.py:431
  265.0 44.8 %collective-permute-start.5 = (bf16[8,6,80,128]{3,2,1,0:T(8,128)(2,1)}, bf16[8,6,80,128]{3,2,1,0:T(8,128)(2,1)}, u32[]{:S(2)}, u32[]{:S(2)}) collective-permute-start(bf16[8,6,80,128]{3,2,1,0:T(8,128)(2,1)} %collective-permute-done.4.refs_1_), channel_id=1, source_target_pairs={{0,7},{1,0},{2,1},{3,2},{4,3},{5,4},{6,5},{7,6},{8,15},{9,8},{10,9... | collective-permute-start | bytes 2949128 | tf_op jit(solution)/shard_map/ppermute | solution.py:432
  309.8 33.0 %collective-permute-start.2 = (bf16[8,6,80,128]{3,2,1,0:T(8,128)(2,1)}, bf16[8,6,80,128]{3,2,1,0:T(8,128)(2,1)}, u32[]{:S(2)}, u32[]{:S(2)}) collective-permute-start(bf16[8,6,80,128]{3,2,1,0:T(8,128)(2,1)} %collective-permute-done.1.refs_0_), channel_id=1, source_target_pairs={{0,1},{1,2},{2,3},{3,4},{4,5},{5,6},{6,7},{7,0},{8,9},{9,10},{10,1... | collective-permute-start | bytes 2949128 | tf_op jit(solution)/shard_map/ppermute | solution.py:431
  309.8 34.9 %collective-permute-start.6 = (bf16[8,6,80,128]{3,2,1,0:T(8,128)(2,1)}, bf16[8,6,80,128]{3,2,1,0:T(8,128)(2,1)}, u32[]{:S(2)}, u32[]{:S(2)}) collective-permute-start(bf16[8,6,80,128]{3,2,1,0:T(8,128)(2,1)} %collective-permute-done.5.refs_1_), channel_id=1, source_target_pairs={{0,7},{1,0},{2,1},{3,2},{4,3},{5,4},{6,5},{7,6},{8,15},{9,8},{10,9... | collective-permute-start | bytes 2949128 | tf_op jit(solution)/shard_map/ppermute | solution.py:432
  312.5 42.6 %collective-permute-start.10 = (bf16[9,6,80,128]{3,2,1,0:T(8,128)(2,1)}, bf16[9,6,80,128]{3,2,1,0:T(8,128)(2,1)S(1)}, u32[]{:S(2)}, u32[]{:S(2)}) collective-permute-start(bf16[9,6,80,128]{3,2,1,0:T(8,128)(2,1)} %collective-permute-done.9.refs_0_.refs_2_), channel_id=1, source_target_pairs={{0,1},{1,2},{2,3},{3,4},{4,5},{5,6},{6,7},{7,0},{8,9},{9,10},{10,1... | collective-permute-start | bytes 3317768 | tf_op jit(solution)/shard_map/ppermute | solution.py:431
  312.5 42.8 %collective-permute-start.14 = (bf16[9,6,80,128]{3,2,1,0:T(8,128)(2,1)}, bf16[9,6,80,128]{3,2,1,0:T(8,128)(2,1)S(1)}, u32[]{:S(2)}, u32[]{:S(2)}) collective-permute-start(bf16[9,6,80,128]{3,2,1,0:T(8,128)(2,1)} %collective-permute-done.13.refs_1_.refs_3_), channel_id=1, source_target_pairs={{0,7},{1,0},{2,1},{3,2},{4,3},{5,4},{6,5},{7,6},{8,15},{9,8},{10,9... | collective-permute-start | bytes 3317768 | tf_op jit(solution)/shard_map/ppermute | solution.py:432
  344.7 40.2 %collective-permute-start.3 = (bf16[8,3,80,128]{3,2,1,0:T(8,128)(2,1)}, bf16[8,3,80,128]{3,2,1,0:T(8,128)(2,1)}, u32[]{:S(2)}, u32[]{:S(2)}) collective-permute-start(bf16[8,3,80,128]{3,2,1,0:T(8,128)(2,1)} %slice.16), channel_id=1, source_target_pairs={{0,1},{1,2},{2,3},{3,4},{4,5},{5,6},{6,7},{7,0},{8,9},{9,10},{10,1... | collective-permute-start | bytes 1474568 | tf_op jit(solution)/shard_map/ppermute | solution.py:431
  346.5 38.3 %collective-permute-start.7 = (bf16[8,3,80,128]{3,2,1,0:T(8,128)(2,1)}, bf16[8,3,80,128]{3,2,1,0:T(8,128)(2,1)}, u32[]{:S(2)}, u32[]{:S(2)}) collective-permute-start(bf16[8,3,80,128]{3,2,1,0:T(8,128)(2,1)} %slice.17), channel_id=1, source_target_pairs={{0,7},{1,0},{2,1},{3,2},{4,3},{5,4},{6,5},{7,6},{8,15},{9,8},{10,9... | collective-permute-start | bytes 1474568 | tf_op jit(solution)/shard_map/ppermute | solution.py:432
  355.1 3.7 copy-start
  355.1 22.3 %collective-permute-start.11 = (bf16[9,3,80,128]{3,2,1,0:T(8,128)(2,1)S(1)}, bf16[9,3,80,128]{3,2,1,0:T(8,128)(2,1)S(1)}, u32[]{:S(2)}, u32[]{:S(2)}) collective-permute-start(bf16[9,3,80,128]{3,2,1,0:T(8,128)(2,1)S(1)} %slice.18), channel_id=1, source_target_pairs={{0,1},{1,2},{2,3},{3,4},{4,5},{5,6},{6,7},{7,0},{8,9},{9,10},{10,1... | collective-permute-start | bytes 1658888 | tf_op jit(solution)/shard_map/ppermute | solution.py:431
  355.3 3.6 copy-start.1
  356.3 21.2 %collective-permute-start.15 = (bf16[9,3,80,128]{3,2,1,0:T(8,128)(2,1)}, bf16[9,3,80,128]{3,2,1,0:T(8,128)(2,1)S(1)}, u32[]{:S(2)}, u32[]{:S(2)}) collective-permute-start(bf16[9,3,80,128]{3,2,1,0:T(8,128)(2,1)} %slice.19), channel_id=1, source_target_pairs={{0,7},{1,0},{2,1},{3,2},{4,3},{5,4},{6,5},{7,6},{8,15},{9,8},{10,9... | collective-permute-start | bytes 1658888 | tf_op jit(solution)/shard_map/ppermute | solution.py:432
  377.5 0.8 copy-start.4
  377.5 1.0 copy-start.5
where the time goes:
time: 398 us; the launch traced here: 391 us
  Pallas kernels  298 us (75%)
  waiting for transfers between devices  64.6 us (16%)
  starting transfers between devices  20.7 us (5%)
  local copies, waits for them, and re-layouts  5.76 us (1%)
    pallas_call x1, Pallas kernels, backward(): pl.pallas_call(functools.partial(backward_kernel, n), out_shape=tuple((ja...  188 us
    pallas_call x10, Pallas kernels, optimizer(): pl.pallas_call(functools.partial(adamw_kernel, len(shards), paired, 1 - l...  80.9 us
    ppermute x8, waiting for transfers between devices, both(): from_left = lax.ppermute(to_right, 'dp', right)  45.1 us
    pallas_call x1, Pallas kernels, forward(): pl.pallas_call(forward_kernel, out_shape=(up, up, across, up, across), gr...  29 us
    ppermute x8, starting transfers between devices, both(): return (from_left, lax.ppermute(to_left, 'dp', left))  20 us
    ppermute x8, waiting for transfers between devices, both(): return (from_left, lax.ppermute(to_left, 'dp', left))  19.5 us
  transfers between devices with their start and end apart: 16, of which 5 were waited for; matrix products, arithmetic and copies ran while one was open for 2% of the time, Pallas kernels for 19%

commit v1 on v0

--- a/solution.py
+++ b/solution.py
@@ -10,9 +10,9 @@
 
 LANES = 128
 FB = 2 * LANES
-K1_ROWS = 512
+F_ROWS = 512
+DOWN_ROWS = 512
 S1_ROWS = 256
-DA_ROWS = 512
 STAGGER = 2
 LEAD = 2
 SLOTS = 12
@@ -46,45 +46,10 @@
     return (w - 0.02 * step).astype(bf16), m, v
 
 
-def forward_kernel(h_ref, wg_ref, wu_ref, wd_ref, h1_ref, a1_ref, a1t_ref, a0_ref, a0t_ref, act_ref):
-    ff = wg_ref.shape[-1]
-    a = normed(h_ref[...])
-    a0_ref[...] = a
-    a0t_ref[...] = a.T
-    for f in range(0, ff, FB):
-        cols = slice(f, min(f + FB, ff))
-        gate, up = dot(a, wg_ref[:, cols]), dot(a, wu_ref[:, cols])
-        act_ref[:, cols] = (gate * jax.nn.sigmoid(gate) * up).astype(bf16)
-    h1 = h_ref[...] + dot(act_ref[...], wd_ref[...]).astype(bf16)
-    h1_ref[...] = h1
-    a1 = normed(h1)
-    a1_ref[...] = a1
-    a1t_ref[...] = a1.T
-
-
-def forward(x, wg, wu, wd):
-    (tokens, d), ff = x.shape, wg.shape[-1]
-    rows = pl.BlockSpec((K1_ROWS, d), lambda i: (i, 0))
-    cols = pl.BlockSpec((d, K1_ROWS), lambda i: (0, i))
-    once = functools.partial(pl.BlockSpec, index_map=lambda i: (0, 0, 0), pipeline_mode=pl.Buffered(1))
-    up, across = jax.ShapeDtypeStruct((tokens, d), bf16), jax.ShapeDtypeStruct((d, tokens), bf16)
-    return pl.pallas_call(
-        forward_kernel,
-        out_shape=(up, up, across, up, across),
-        grid=(tokens // K1_ROWS,),
-        in_specs=[rows, once((None, d, ff)), once((None, d, ff)), once((None, ff, d))],
-        out_specs=(rows, rows, cols, rows, cols),
-        scratch_shapes=[pltpu.VMEM((K1_ROWS, ff), bf16)],
-        compiler_params=pltpu.CompilerParams(vmem_limit_bytes=56 * MIB),
-        cost_estimate=pl.CostEstimate(flops=6 * tokens * d * ff, bytes_accessed=8 * d * ff, transcendentals=0),
-        name="forward0",
-    )(x, wg, wu, wd)
-
-
-def backward_kernel(n, *refs):
-    (a1, a1t, dy, h1, a0, a0t, wg, wu, wd, *out_refs), refs = refs[:11], refs[11:]
-    (av, atv, dv, dgv, duv, actv, wgr, wur, wdr, wgf, wuf, hv, g_ref, ra, rb) = refs[:15]
-    (sem_w, sem_in, sem_full, sem_h, sem_sa, sem_ra, sem_sb, sem_rb, free_a, free_b, sem_out) = refs[15:]
+def train_kernel(n, *refs):
+    (x, dy, wg, wu, wd, *out_refs), refs = refs[:7], refs[7:]
+    (av, atv, dv, dgv, duv, actv, wgr, wur, wdr, wgf, wuf, hv, h1v, g_ref, ra, rb) = refs[:16]
+    (sem_w, sem_in, sem_down, sem_full, sem_x, sem_sa, sem_ra, sem_sb, sem_rb, free_a, free_b, sem_out) = refs[16:]
     tokens, d = av.shape
     ff = wg.shape[-1]
     units, lanes = g_ref.shape[:2]
@@ -217,7 +182,7 @@
         return k * pace[0] // pace[1]
 
     first = (ALONE - 1) * rounds + paced(PACE[0], POINTS * (blocks - ALONE))
-    later = first + paced(PACE[1], tokens // DA_ROWS)
+    later = first + paced(PACE[1], tokens // F_ROWS)
     finish = later + paced(PACE[2], POINTS * blocks)
 
     def served(b, i):
@@ -247,9 +212,16 @@
 
     loads = [
         pltpu.make_async_copy(src, dst, sem_in.at[i])
-        for i, (src, dst) in enumerate(((a1, av), (dy, dv), (a1t, atv)))
+        for i, (src, dst) in enumerate(((wg.at[0], dgv.at[pl.ds(0, d)]), (wu.at[0], dgv.at[pl.ds(d, d)]), (dy, dv)))
     ]
-    second = [pltpu.make_async_copy(src, dst, sem_in.at[i]) for i, (src, dst) in enumerate(((a0, av), (a0t, atv)))]
+    runs = [(i, f, min(DOWN_ROWS, ff - f)) for i, f in enumerate(range(0, ff, DOWN_ROWS))]
+    downs = [
+        pltpu.make_async_copy(
+            wd.at[0, pl.ds(f, many), pl.ds(c * LANES, LANES)], g_ref.at[i, c, pl.ds(0, many)], sem_down.at[i, c]
+        )
+        for i, f, many in runs
+        for c in range(d // LANES)
+    ]
     whole = [pltpu.make_async_copy(src.at[1], dst, sem_full.at[i]) for i, (src, dst) in enumerate(((wg, wgf), (wu, wuf)))]
 
     def place(b):
@@ -266,40 +238,71 @@
             pltpu.make_async_copy(wd.at[layer, pl.ds(c, FB), :], wdr.at[s], sem_w.at[2, s]),
         )
 
-    for copy in (*weights(jnp.int32(0)), *loads[:2]):
+    def x_tile(t):
+        at = pl.ds(pl.multiple_of(t * F_ROWS, F_ROWS), F_ROWS)
+        return pltpu.make_async_copy(x.at[at], hv.at[lax.rem(t, 2)], sem_x.at[lax.rem(t, 2)])
+
+    def next_x(t):
+        @pl.when(t + 1 < tokens // F_ROWS)
+        def _():
+            x_tile(t + 1).start()
+
+        x_tile(t).wait()
+
+    tiles = tokens // F_ROWS
+
+    def normalize(t):
+        r = pl.ds(pl.multiple_of(t * F_ROWS, F_ROWS), F_ROWS)
+        a = normed(h1v[r, :])
+        av[r, :] = a
+        atv[:, r] = a.T
+
+    def forward(t, carry):
+        r = pl.ds(pl.multiple_of(t * F_ROWS, F_ROWS), F_ROWS)
+        next_x(t)
+        normalize(lax.rem(t + tiles - 1, tiles))
+        h = hv[lax.rem(t, 2)]
+        a = normed(h)
+        for f in range(0, ff, FB):
+            cols = slice(f, min(f + FB, ff))
+            gate, up = dot(a, dgv[:d, cols]), dot(a, dgv[d : 2 * d, cols])
+            duv[:F_ROWS, cols] = (gate * jax.nn.sigmoid(gate) * up).astype(bf16)
+        down = sum(
+            dot(duv[:F_ROWS, f : f + many], jnp.concatenate([g_ref[i, c, :many] for c in range(d // LANES)], 1))
+            for i, f, many in runs
+        )
+        h = h + down.astype(bf16)
+        h1v[r, :] = h
+        return carry
+
+    x_tile(jnp.int32(0)).start()
+    for copy in (*loads[:2], *downs, loads[2], *weights(jnp.int32(0))):
         copy.start()
     barrier = pltpu.get_barrier_semaphore()
     for neighbour in (left, right):
         pl.semaphore_signal(barrier, inc=1, device_id={"dp": neighbour}, device_id_type=MESH)
-    for copy in loads[2:]:
-        copy.start()
-    for copy in loads[:2]:
+    for copy in (*loads[:2], *downs):
         copy.wait()
+    lax.fori_loop(0, tiles, forward, 0)
+    normalize(tiles - 1)
+    loads[2].wait()
     pl.semaphore_wait(barrier, 2)
 
-    def h_tile(t):
-        return pltpu.make_async_copy(h1.at[pl.ds(t * DA_ROWS, DA_ROWS)], hv.at[lax.rem(t, 2)], sem_h.at[lax.rem(t, 2)])
-
     def through_norm():
-        da_tiles = tokens // DA_ROWS
-        for copy in second:
-            copy.start()
         for copy in whole:
             copy.wait()
-        h_tile(jnp.int32(0)).start()
+        x_tile(jnp.int32(0)).start()
 
         def tile(t, carry):
-            r = pl.ds(pl.multiple_of(t * DA_ROWS, DA_ROWS), DA_ROWS)
-
-            @pl.when(t + 1 < da_tiles)
-            def _():
-                h_tile(t + 1).start()
-
-            h_tile(t).wait()
+            r = pl.ds(pl.multiple_of(t * F_ROWS, F_ROWS), F_ROWS)
+            next_x(t)
+            a = normed(hv[lax.rem(t, 2)])
+            av[r, :] = a
+            atv[:, r] = a.T
             last = ((1,), (1,))
             da = wide(dot(dgv[r, :], wgf[...], last).astype(bf16)) + wide(dot(duv[r, :], wuf[...], last).astype(bf16))
             da = wide(da.astype(bf16))
-            h = wide(hv[lax.rem(t, 2)])
+            h = wide(h1v[r, :])
             scale = lax.rsqrt(jnp.mean(h * h, -1, keepdims=True) + 1e-6)
             dh = (da * scale - h * (scale * scale * scale * jnp.mean(da * h, -1, keepdims=True))).astype(bf16)
             dh = (wide(dv[r, :]) + wide(dh)).astype(bf16)
@@ -307,9 +310,7 @@
             serve_all(first + paced(PACE[1], t), first + paced(PACE[1], t + 1), full)
             return carry
 
-        lax.fori_loop(0, da_tiles, tile, 0)
-        for copy in second:
-            copy.wait()
+        lax.fori_loop(0, tokens // F_ROWS, tile, 0)
 
     def block(b, carry):
         layer, j, c = place(b)
@@ -353,11 +354,6 @@
                 before = (r, *made)
             pointwise(*before)
             point(b, i)
-
-        @pl.when(b == 0)
-        def _():
-            for copy in loads[2:]:
-                copy.wait()
 
         rest = j == full
         u = jnp.where(rest, units - 1, jnp.where(layer == 1, j, full + j))
@@ -398,30 +394,31 @@
     lax.fori_loop(0, units, written, 0)
 
 
-def backward(n, a1, a1t, dy, h1, a0, a0t, wg, wu, wd):
-    (tokens, d), (layers, _, ff) = a1.shape, wg.shape
+def train(n, x, dy, wg, wu, wd):
+    (tokens, d), (layers, _, ff) = x.shape, wg.shape
     full, lanes = ff // FB, 3 * FB // LANES
     units = layers * full + 1
-    assert layers == 2 and ff % FB == LANES and d % (16 * n) == 0 and LANES // n * (d // LANES) == d // n
+    assert layers == 2 and 2 * d <= tokens and ff % FB == LANES and d % (16 * n) == 0 and LANES // n * (d // LANES) == d // n
+    assert DOWN_ROWS <= d and -(-ff // DOWN_ROWS) <= units and d // LANES <= lanes
     assert SLOTS % (n // 2) == 0 and LEAD + 1 <= SLOTS // (n // 2)
     dma, vmem = pltpu.SemaphoreType.DMA, lambda *shape: pltpu.VMEM(shape, bf16)
     return pl.pallas_call(
-        functools.partial(backward_kernel, n),
+        functools.partial(train_kernel, n),
         out_shape=tuple(jax.ShapeDtypeStruct((size, lanes, d // n, LANES), bf16) for size in (full + 1, full)),
-        in_specs=[ANY] * 9,
+        in_specs=[ANY] * 5,
         out_specs=(ANY,) * 2,
         scratch_shapes=[
             vmem(tokens, d), vmem(d, tokens), vmem(tokens, d), vmem(tokens, ff), vmem(tokens, ff),
             vmem(tokens, FB), vmem(2, d, FB), vmem(2, d, FB), vmem(2, FB, d), vmem(d, ff), vmem(d, ff),
-            vmem(2, DA_ROWS, d), vmem(units, lanes, d, LANES),
+            vmem(2, F_ROWS, d), vmem(tokens, d), vmem(units, lanes, d, LANES),
             vmem(SLOTS, lanes, d // n, LANES), vmem(SLOTS, lanes, d // n, LANES),
-            dma((3, 2)), dma((3,)), dma((2,)), dma((2,)), dma((SLOTS,)), dma((SLOTS,)), dma((SLOTS,)), dma((SLOTS,)),
+            dma((3, 2)), dma((3,)), dma((-(-ff // DOWN_ROWS), d // LANES)), dma((2,)), dma((2,)), dma((SLOTS,)), dma((SLOTS,)), dma((SLOTS,)), dma((SLOTS,)),
             pltpu.SemaphoreType.REGULAR((SLOTS,)), pltpu.SemaphoreType.REGULAR((SLOTS,)), dma((units,)),
         ],
         compiler_params=pltpu.CompilerParams(collective_id=0, has_side_effects=True, vmem_limit_bytes=67043328),
-        cost_estimate=pl.CostEstimate(flops=24 * tokens * d * ff, bytes_accessed=40 * d * ff, transcendentals=0),
-        name="backward_reduce",
-    )(a1, a1t, dy, h1, a0, a0t, wg, wu, wd)
+        cost_estimate=pl.CostEstimate(flops=30 * tokens * d * ff, bytes_accessed=40 * d * ff, transcendentals=0),
+        name="train",
+    )(x, dy, wg, wu, wd)
 
 
 def gather(n, mine):
@@ -520,8 +517,7 @@
     def step(x, dy, *arrays):
         wg, wu, wd = arrays[:3]
         x, dy = x[0], dy[0]
-        h1, a1, a1t, a0, a0t = forward(x, wg, wu, wd)
-        second, first = backward(n, a1, a1t, dy, h1, a0, a0t, wg, wu, wd)
+        second, first = train(n, x, dy, wg, wu, wd)
         me = lax.axis_index("dp").astype(jnp.int32)[None]
         shapes = [a.shape for a in arrays]
         arrays = [a.reshape(a.shape[0], -1, LANES, a.shape[2]) if i % 3 == 2 else a for i, a in enumerate(arrays)]

time: 398 us -> 392 us (0.985)
  Pallas kernels: 298 us -> 292 us
    pallas_call x2 -> x1, Pallas kernels: 217 us -> 211 us  [train(): pl.pallas_call(functools.partial(train_kernel, n), out_shape=tuple((jax.S...]
where the time goes in v1:
time: 392 us; the launch traced here: 386 us
  Pallas kernels  292 us (74%)
  waiting for transfers between devices  64.5 us (16%)
  starting transfers between devices  20.6 us (5%)
  local copies, waits for them, and re-layouts  5.76 us (1%)
    pallas_call x1, Pallas kernels, train(): pl.pallas_call(functools.partial(train_kernel, n), out_shape=tuple((jax.S...  211 us
    pallas_call x10, Pallas kernels, optimizer(): pl.pallas_call(functools.partial(adamw_kernel, len(shards), paired, 1 - l...  80.9 us
    ppermute x8, waiting for transfers between devices, both(): from_left = lax.ppermute(to_right, 'dp', right)  45 us
    ppermute x8, starting transfers between devices, both(): return (from_left, lax.ppermute(to_left, 'dp', left))  20 us
    ppermute x8, waiting for transfers between devices, both(): return (from_left, lax.ppermute(to_left, 'dp', left))  19.5 us
  transfers between devices with their start and end apart: 16, of which 5 were waited for; matrix products, arithmetic and copies ran while one was open for 2% of the time, Pallas kernels for 19%

profile of v1, /device:TPU:21, one launch (start us, length us, event | category | flops | bytes accessed | tf_op | source)
XLA Modules:
  0.0 385.7 jit_solution(5803957441180827071)
XLA Ops:
  0.6 211.1 %train.1 = (bf16[9,6,80,128]{3,2,1,0:T(8,128)(2,1)}, bf16[8,6,80,128]{3,2,1,0:T(8,128)(2,1)}) custom-call(bf16[2048,640]{1,0:T(8,128)(2,1)} %bitcast.42, bf16[2048,640]{1,0:T(8,128)(2,1)} %bitcast.43, bf16[2,640,2176]{2,1,0:T(8,128)(2,1)} %refs_4_.11, bf16[2,640,2176]{2,1,0:T(8,128)(2,1)} %refs_5_.19, bf16[2,2176,640]{2,1,0:T(8,128)(2,1)} %refs_4_.6), custom_call_target="tpu_custom_call" | custom-call | flops 85563801600 | bytes 55705600 | tf_op jit(solution)/shard_map/train/pallas_call | solution.py:405
  211.7 1.4 collective-permute-start.12
  213.2 0.1 collective-permute-start.8
  213.3 0.4 collective-permute-start
  213.7 2.3 collective-permute-start.4
  216.0 19.5 %collective-permute-done.12.refs_1_.refs_3_ = bf16[9,6,80,128]{3,2,1,0:T(8,128)(2,1)S(1)} collective-permute-done((bf16[9,6,80,128]{3,2,1,0:T(8,128)(2,1)}, bf16[9,6,80,128]{3,2,1,0:T(8,128)(2,1)S(1)}, u32[]{:S(2)}, u32[]{:S(2)}) %collective-permute-start.12) | collective-permute-done | bytes 1105952 | tf_op jit(solution)/shard_map/ppermute | solution.py:429
  235.5 0.0 copy-start.2
  235.5 3.1 collective-permute-start.13
  238.5 0.0 collective-permute-done.8.refs_0_.refs_2_
  238.5 0.0 copy-start.3
  238.5 0.0 collective-permute-start.9
  238.6 0.7 pad_add_fusion.2.ids_ref
  239.3 20.1 %collective-permute-done.refs_0_ = bf16[8,6,80,128]{3,2,1,0:T(8,128)(2,1)} collective-permute-done((bf16[8,6,80,128]{3,2,1,0:T(8,128)(2,1)}, bf16[8,6,80,128]{3,2,1,0:T(8,128)(2,1)}, u32[]{:S(2)}, u32[]{:S(2)}) %collective-permute-start) | collective-permute-done | bytes 983072 | tf_op jit(solution)/shard_map/ppermute | solution.py:428
  259.4 0.0 collective-permute-start.1
  259.4 0.0 collective-permute-done.4.refs_1_
  259.4 2.7 collective-permute-start.5
  262.1 0.6 pad_add_fusion.1.ids_ref
  262.7 0.7 pad_add_fusion.ids_ref
  263.4 6.4 %adamw.10 = (bf16[2,640,2176]{2,1,0:T(8,128)(2,1)}, bf16[2,640,2176]{2,1,0:T(8,128)(2,1)}, bf16[2,17,128,640]{3,2,1,0:T(8,128)(2,1)}, f32[2,640,2176]{2,1,0:T(8,...) custom-call(s32[1]{0:T(128)S(6)} %rem.159.ids_ref, ...), custom_call_target="tpu_custom_call" | custom-call | flops 2088960000 | bytes 11489280 | tf_op jit(solution)/shard_map/adamw/pallas_call | solution.py:499
  269.7 0.0 copy-done.2
  269.7 0.0 copy-done.3
  269.7 6.5 %adamw.11 = (bf16[2,640,2176]{2,1,0:T(8,128)(2,1)}, bf16[2,640,2176]{2,1,0:T(8,128)(2,1)}, bf16[2,17,128,640]{3,2,1,0:T(8,128)(2,1)}, f32[2,640,2176]{2,1,0:T(8,...) custom-call(s32[1]{0:T(128)S(6)} %rem.159.ids_ref, ...), custom_call_target="tpu_custom_call", output_to_operand_aliasing={{0}: (12, {}), {1}: (13, {}), {2}: (14, {}), {3}: (15, {}),... | custom-call | flops 2088960000 | bytes 11489280 | tf_op jit(solution)/shard_map/adamw/pallas_call | solution.py:499
  276.2 9.2 %adamw.12 = (bf16[2,640,2176]{2,1,0:T(8,128)(2,1)}, bf16[2,640,2176]{2,1,0:T(8,128)(2,1)}, bf16[2,17,128,640]{3,2,1,0:T(8,128)(2,1)}, f32[2,640,2176]{2,1,0:T(8,...) custom-call(s32[2]{0:T(128)} %pad_add_fusion.2.ids_ref, ...), custom_call_target="tpu_custom_call", output_to_operand_aliasing={{0}: (12, {}), {1}: (13, {}), {2}: (14, {}), {3}: (15, {}),... | custom-call | flops 4177920000 | bytes 22978560 | tf_op jit(solution)/shard_map/adamw/pallas_call | solution.py:499
  285.4 18.8 %collective-permute-done.1.refs_0_ = bf16[8,6,80,128]{3,2,1,0:T(8,128)(2,1)} collective-permute-done((bf16[8,6,80,128]{3,2,1,0:T(8,128)(2,1)}, bf16[8,6,80,128]{3,2,1,0:T(8,128)(2,1)}, u32[]{:S(2)}, u32[]{:S(2)}) %collective-permute-start.1) | collective-permute-done | bytes 983072 | tf_op jit(solution)/shard_map/ppermute | solution.py:428
  304.2 0.0 collective-permute-start.2
  304.2 0.0 collective-permute-done.5.refs_1_
  304.2 0.0 copy-start.6
  304.2 2.7 collective-permute-start.6
  306.9 0.0 collective-permute-done.9.refs_0_.refs_2_
  306.9 0.0 collective-permute-start.10
  306.9 0.0 collective-permute-done.13.refs_1_.refs_3_
  306.9 2.7 collective-permute-start.14
  309.6 9.1 %adamw.13 = (bf16[2,640,2176]{2,1,0:T(8,128)(2,1)}, bf16[2,640,2176]{2,1,0:T(8,128)(2,1)}, bf16[2,17,128,640]{3,2,1,0:T(8,128)(2,1)}, f32[2,640,2176]{2,1,0:T(8,...) custom-call(s32[2]{0:T(128)} %pad_add_fusion.2.ids_ref, ...), custom_call_target="tpu_custom_call", output_to_operand_aliasing={{0}: (14, {}), {1}: (15, {}), {2}: (16, {}), {3}: (17, {}),... | custom-call | flops 4177920000 | bytes 22978560 | tf_op jit(solution)/shard_map/adamw/pallas_call | solution.py:499
  318.7 0.0 copy-done.6
  318.7 9.3 %adamw.14 = (bf16[2,640,2176]{2,1,0:T(8,128)(2,1)}, bf16[2,640,2176]{2,1,0:T(8,128)(2,1)}, bf16[2,17,128,640]{3,2,1,0:T(8,128)(2,1)}, f32[2,640,2176]{2,1,0:T(8,...) custom-call(s32[2]{0:T(128)} %pad_add_fusion.1.ids_ref, ...), custom_call_target="tpu_custom_call", output_to_operand_aliasing={{0}: (12, {}), {1}: (13, {}), {2}: (14, {}), {3}: (15, {}),... | custom-call | flops 4177920000 | bytes 22978560 | tf_op jit(solution)/shard_map/adamw/pallas_call | solution.py:499
  328.0 9.2 %adamw.15 = (bf16[2,640,2176]{2,1,0:T(8,128)(2,1)}, bf16[2,640,2176]{2,1,0:T(8,128)(2,1)}, bf16[2,17,128,640]{3,2,1,0:T(8,128)(2,1)}, f32[2,640,2176]{2,1,0:T(8,...) custom-call(s32[2]{0:T(128)} %pad_add_fusion.1.ids_ref, ...), custom_call_target="tpu_custom_call", output_to_operand_aliasing={{0}: (14, {}), {1}: (15, {}), {2}: (16, {}), {3}: (17, {}),... | custom-call | flops 4177920000 | bytes 22978560 | tf_op jit(solution)/shard_map/adamw/pallas_call | solution.py:499
  337.2 0.0 collective-permute-done.2.refs_0_
  337.2 1.8 slice.16
  339.1 0.0 collective-permute-start.3
  339.1 0.0 collective-permute-done.6.refs_1_
  339.1 1.8 slice.17
  340.9 2.7 collective-permute-start.7
  343.6 5.9 %collective-permute-done.10.refs_0_.refs_2_ = bf16[9,6,80,128]{3,2,1,0:T(8,128)(2,1)S(1)} collective-permute-done((bf16[9,6,80,128]{3,2,1,0:T(8,128)(2,1)}, bf16[9,6,80,128]{3,2,1,0:T(8,128)(2,1)S(1)}, u32[]{:S(2)}, u32[]{:S(2)}) %collective-permute-start.10) | collective-permute-done | bytes 1105952 | tf_op jit(solution)/shard_map/ppermute | solution.py:428
  349.5 0.0 copy-start
  349.5 0.1 collective-permute-start.11
  349.6 0.0 collective-permute-done.14.refs_1_.refs_3_
  349.7 0.0 copy-start.1
  349.7 1.0 slice.19
  350.7 2.5 collective-permute-start.15
  353.2 0.0 copy-done
  353.2 0.0 copy-done.1
  353.2 9.2 %adamw.16 = (bf16[2,640,2176]{2,1,0:T(8,128)(2,1)}, bf16[2,640,2176]{2,1,0:T(8,128)(2,1)}, bf16[2,17,128,640]{3,2,1,0:T(8,128)(2,1)}, f32[2,640,2176]{2,1,0:T(8,...) custom-call(s32[2]{0:T(128)} %pad_add_fusion.ids_ref, ...), custom_call_target="tpu_custom_call", output_to_operand_aliasing={{0}: (12, {}), {1}: (13, {}), {2}: (14, {}), {3}: (15, {}),... | custom-call | flops 4177920000 | bytes 22978560 | tf_op jit(solution)/shard_map/adamw/pallas_call | solution.py:499
  362.4 9.2 %adamw.17 = (bf16[2,640,2176]{2,1,0:T(8,128)(2,1)}, bf16[2,640,2176]{2,1,0:T(8,128)(2,1)}, bf16[2,17,128,640]{3,2,1,0:T(8,128)(2,1)}, f32[2,640,2176]{2,1,0:T(8,...) custom-call(s32[2]{0:T(128)} %pad_add_fusion.ids_ref, ...), custom_call_target="tpu_custom_call", output_to_operand_aliasing={{0}: (14, {}), {1}: (15, {}), {2}: (16, {}), {3}: (17, {}),... | custom-call | flops 4177920000 | bytes 22978560 | tf_op jit(solution)/shard_map/adamw/pallas_call | solution.py:499
  371.7 0.2 collective-permute-done.11.refs_0_.refs_2_
  371.9 0.0 copy-start.4
  371.9 0.0 collective-permute-done.15.refs_1_.refs_3_
  371.9 0.0 copy-start.5
  371.9 0.8 copy-done.4
  372.7 0.2 copy-done.5
  372.9 6.4 %adamw.18 = (bf16[2,640,2176]{2,1,0:T(8,128)(2,1)}, bf16[2,640,2176]{2,1,0:T(8,128)(2,1)}, bf16[2,17,128,640]{3,2,1,0:T(8,128)(2,1)}, f32[2,640,2176]{2,1,0:T(8,...) custom-call(s32[1]{0:T(128)S(6)} %rem.117.ids_ref, ...), custom_call_target="tpu_custom_call", output_to_operand_aliasing={{0}: (12, {}), {1}: (13, {}), {2}: (14, {}), {3}: (15, {}),... | custom-call | flops 2088960000 | bytes 11489280 | tf_op jit(solution)/shard_map/adamw/pallas_call | solution.py:499
  379.2 0.0 collective-permute-done.3.refs_0_
  379.2 0.0 collective-permute-done.7.refs_1_
  379.2 6.4 %adamw.19 = (bf16[2,640,2176]{2,1,0:T(8,128)(2,1)}, bf16[2,640,2176]{2,1,0:T(8,128)(2,1)}, bf16[2,17,128,640]{3,2,1,0:T(8,128)(2,1)}, f32[2,640,2176]{2,1,0:T(8,...) custom-call(s32[1]{0:T(128)S(6)} %rem.117.ids_ref, ...), custom_call_target="tpu_custom_call", output_to_operand_aliasing={{0}: (14, {}), {1}: (15, {}), {2}: (16, {}), {3}: (17, {}),... | custom-call | flops 2088960000 | bytes 11489280 | tf_op jit(solution)/shard_map/adamw/pallas_call | solution.py:499
  (1 shorter events, 0.0 us)
Async XLA Ops:
  211.7 23.7 %collective-permute-start.12 = (bf16[9,6,80,128]{3,2,1,0:T(8,128)(2,1)}, bf16[9,6,80,128]{3,2,1,0:T(8,128)(2,1)S(1)}, u32[]{:S(2)}, u32[]{:S(2)}) collective-permute-start(bf16[9,6,80,128]{3,2,1,0:T(8,128)(2,1)} %get-tuple-element.102.refs_0_.refs_1_), channel_id=1, source_target_pairs={{0,7},{1,0},{2,1},{3,2},{4,3},{5,4},{6,5},{7,6},{8,15},{9,8},{10,9... | collective-permute-start | bytes 3317768 | tf_op jit(solution)/shard_map/ppermute | solution.py:429
  213.2 25.4 %collective-permute-start.8 = (bf16[9,6,80,128]{3,2,1,0:T(8,128)(2,1)}, bf16[9,6,80,128]{3,2,1,0:T(8,128)(2,1)S(1)}, u32[]{:S(2)}, u32[]{:S(2)}) collective-permute-start(bf16[9,6,80,128]{3,2,1,0:T(8,128)(2,1)} %get-tuple-element.102.refs_0_.refs_1_), channel_id=1, source_target_pairs={{0,1},{1,2},{2,3},{3,4},{4,5},{5,6},{6,7},{7,0},{8,9},{9,10},{10,1... | collective-permute-start | bytes 3317768 | tf_op jit(solution)/shard_map/ppermute | solution.py:428
  213.3 46.1 %collective-permute-start = (bf16[8,6,80,128]{3,2,1,0:T(8,128)(2,1)}, bf16[8,6,80,128]{3,2,1,0:T(8,128)(2,1)}, u32[]{:S(2)}, u32[]{:S(2)}) collective-permute-start(bf16[8,6,80,128]{3,2,1,0:T(8,128)(2,1)} %get-tuple-element.101.refs_0_), channel_id=1, source_target_pairs={{0,1},{1,2},{2,3},{3,4},{4,5},{5,6},{6,7},{7,0},{8,9},{9,10},{10,1... | collective-permute-start | bytes 2949128 | tf_op jit(solution)/shard_map/ppermute | solution.py:428
  213.7 45.7 %collective-permute-start.4 = (bf16[8,6,80,128]{3,2,1,0:T(8,128)(2,1)}, bf16[8,6,80,128]{3,2,1,0:T(8,128)(2,1)}, u32[]{:S(2)}, u32[]{:S(2)}) collective-permute-start(bf16[8,6,80,128]{3,2,1,0:T(8,128)(2,1)} %get-tuple-element.101.refs_0_), channel_id=1, source_target_pairs={{0,7},{1,0},{2,1},{3,2},{4,3},{5,4},{6,5},{7,6},{8,15},{9,8},{10,9... | collective-permute-start | bytes 2949128 | tf_op jit(solution)/shard_map/ppermute | solution.py:429
  235.5 34.3 %copy-start.2 = (bf16[9,6,80,128]{3,2,1,0:T(8,128)(2,1)}, bf16[9,6,80,128]{3,2,1,0:T(8,128)(2,1)S(1)}, u32[]{:S(2)}) copy-start(bf16[9,6,80,128]{3,2,1,0:T(8,128)(2,1)S(1)} %collective-permute-done.12.refs_1_.refs_3_) | copy-start | bytes 3317764
  235.5 71.4 %collective-permute-start.13 = (bf16[9,6,80,128]{3,2,1,0:T(8,128)(2,1)S(1)}, bf16[9,6,80,128]{3,2,1,0:T(8,128)(2,1)}, u32[]{:S(2)}, u32[]{:S(2)}) collective-permute-start(bf16[9,6,80,128]{3,2,1,0:T(8,128)(2,1)S(1)} %collective-permute-done.12.refs_1_.refs_3_), channel_id=1, source_target_pairs={{0,7},{1,0},{2,1},{3,2},{4,3},{5,4},{6,5},{7,6},{8,15},{9,8},{10,9... | collective-permute-start | bytes 3317768 | tf_op jit(solution)/shard_map/ppermute | solution.py:429
  238.5 31.2 %copy-start.3 = (bf16[9,6,80,128]{3,2,1,0:T(8,128)(2,1)}, bf16[9,6,80,128]{3,2,1,0:T(8,128)(2,1)S(1)}, u32[]{:S(2)}) copy-start(bf16[9,6,80,128]{3,2,1,0:T(8,128)(2,1)S(1)} %collective-permute-done.8.refs_0_.refs_2_) | copy-start | bytes 3317764
  238.5 68.3 %collective-permute-start.9 = (bf16[9,6,80,128]{3,2,1,0:T(8,128)(2,1)S(1)}, bf16[9,6,80,128]{3,2,1,0:T(8,128)(2,1)}, u32[]{:S(2)}, u32[]{:S(2)}) collective-permute-start(bf16[9,6,80,128]{3,2,1,0:T(8,128)(2,1)S(1)} %collective-permute-done.8.refs_0_.refs_2_), channel_id=1, source_target_pairs={{0,1},{1,2},{2,3},{3,4},{4,5},{5,6},{6,7},{7,0},{8,9},{9,10},{10,1... | collective-permute-start | bytes 3317768 | tf_op jit(solution)/shard_map/ppermute | solution.py:428
  259.4 44.8 %collective-permute-start.1 = (bf16[8,6,80,128]{3,2,1,0:T(8,128)(2,1)}, bf16[8,6,80,128]{3,2,1,0:T(8,128)(2,1)}, u32[]{:S(2)}, u32[]{:S(2)}) collective-permute-start(bf16[8,6,80,128]{3,2,1,0:T(8,128)(2,1)} %collective-permute-done.refs_0_), channel_id=1, source_target_pairs={{0,1},{1,2},{2,3},{3,4},{4,5},{5,6},{6,7},{7,0},{8,9},{9,10},{10,1... | collective-permute-start | bytes 2949128 | tf_op jit(solution)/shard_map/ppermute | solution.py:428
  259.4 44.8 %collective-permute-start.5 = (bf16[8,6,80,128]{3,2,1,0:T(8,128)(2,1)}, bf16[8,6,80,128]{3,2,1,0:T(8,128)(2,1)S(1)}, u32[]{:S(2)}, u32[]{:S(2)}) collective-permute-start(bf16[8,6,80,128]{3,2,1,0:T(8,128)(2,1)} %collective-permute-done.4.refs_1_), channel_id=1, source_target_pairs={{0,7},{1,0},{2,1},{3,2},{4,3},{5,4},{6,5},{7,6},{8,15},{9,8},{10,9... | collective-permute-start | bytes 2949128 | tf_op jit(solution)/shard_map/ppermute | solution.py:429
  304.2 33.0 %collective-permute-start.2 = (bf16[8,6,80,128]{3,2,1,0:T(8,128)(2,1)}, bf16[8,6,80,128]{3,2,1,0:T(8,128)(2,1)}, u32[]{:S(2)}, u32[]{:S(2)}) collective-permute-start(bf16[8,6,80,128]{3,2,1,0:T(8,128)(2,1)} %collective-permute-done.1.refs_0_), channel_id=1, source_target_pairs={{0,1},{1,2},{2,3},{3,4},{4,5},{5,6},{6,7},{7,0},{8,9},{9,10},{10,1... | collective-permute-start | bytes 2949128 | tf_op jit(solution)/shard_map/ppermute | solution.py:428
  304.2 14.5 %copy-start.6 = (bf16[8,6,80,128]{3,2,1,0:T(8,128)(2,1)}, bf16[8,6,80,128]{3,2,1,0:T(8,128)(2,1)S(1)}, u32[]{:S(2)}) copy-start(bf16[8,6,80,128]{3,2,1,0:T(8,128)(2,1)S(1)} %collective-permute-done.5.refs_1_) | copy-start | bytes 2949124
  304.2 34.9 %collective-permute-start.6 = (bf16[8,6,80,128]{3,2,1,0:T(8,128)(2,1)S(1)}, bf16[8,6,80,128]{3,2,1,0:T(8,128)(2,1)}, u32[]{:S(2)}, u32[]{:S(2)}) collective-permute-start(bf16[8,6,80,128]{3,2,1,0:T(8,128)(2,1)S(1)} %collective-permute-done.5.refs_1_), channel_id=1, source_target_pairs={{0,7},{1,0},{2,1},{3,2},{4,3},{5,4},{6,5},{7,6},{8,15},{9,8},{10,9... | collective-permute-start | bytes 2949128 | tf_op jit(solution)/shard_map/ppermute | solution.py:429
  306.9 42.6 %collective-permute-start.10 = (bf16[9,6,80,128]{3,2,1,0:T(8,128)(2,1)}, bf16[9,6,80,128]{3,2,1,0:T(8,128)(2,1)S(1)}, u32[]{:S(2)}, u32[]{:S(2)}) collective-permute-start(bf16[9,6,80,128]{3,2,1,0:T(8,128)(2,1)} %collective-permute-done.9.refs_0_.refs_2_), channel_id=1, source_target_pairs={{0,1},{1,2},{2,3},{3,4},{4,5},{5,6},{6,7},{7,0},{8,9},{9,10},{10,1... | collective-permute-start | bytes 3317768 | tf_op jit(solution)/shard_map/ppermute | solution.py:428
  306.9 42.8 %collective-permute-start.14 = (bf16[9,6,80,128]{3,2,1,0:T(8,128)(2,1)}, bf16[9,6,80,128]{3,2,1,0:T(8,128)(2,1)S(1)}, u32[]{:S(2)}, u32[]{:S(2)}) collective-permute-start(bf16[9,6,80,128]{3,2,1,0:T(8,128)(2,1)} %collective-permute-done.13.refs_1_.refs_3_), channel_id=1, source_target_pairs={{0,7},{1,0},{2,1},{3,2},{4,3},{5,4},{6,5},{7,6},{8,15},{9,8},{10,9... | collective-permute-start | bytes 3317768 | tf_op jit(solution)/shard_map/ppermute | solution.py:429
  339.1 40.1 %collective-permute-start.3 = (bf16[8,3,80,128]{3,2,1,0:T(8,128)(2,1)}, bf16[8,3,80,128]{3,2,1,0:T(8,128)(2,1)}, u32[]{:S(2)}, u32[]{:S(2)}) collective-permute-start(bf16[8,3,80,128]{3,2,1,0:T(8,128)(2,1)} %slice.16), channel_id=1, source_target_pairs={{0,1},{1,2},{2,3},{3,4},{4,5},{5,6},{6,7},{7,0},{8,9},{9,10},{10,1... | collective-permute-start | bytes 1474568 | tf_op jit(solution)/shard_map/ppermute | solution.py:428
  340.9 38.3 %collective-permute-start.7 = (bf16[8,3,80,128]{3,2,1,0:T(8,128)(2,1)}, bf16[8,3,80,128]{3,2,1,0:T(8,128)(2,1)}, u32[]{:S(2)}, u32[]{:S(2)}) collective-permute-start(bf16[8,3,80,128]{3,2,1,0:T(8,128)(2,1)} %slice.17), channel_id=1, source_target_pairs={{0,7},{1,0},{2,1},{3,2},{4,3},{5,4},{6,5},{7,6},{8,15},{9,8},{10,9... | collective-permute-start | bytes 1474568 | tf_op jit(solution)/shard_map/ppermute | solution.py:429
  349.5 3.7 copy-start
  349.5 22.3 %collective-permute-start.11 = (bf16[9,3,80,128]{3,2,1,0:T(8,128)(2,1)S(1)}, bf16[9,3,80,128]{3,2,1,0:T(8,128)(2,1)S(1)}, u32[]{:S(2)}, u32[]{:S(2)}) collective-permute-start(bf16[9,3,80,128]{3,2,1,0:T(8,128)(2,1)S(1)} %slice.18), channel_id=1, source_target_pairs={{0,1},{1,2},{2,3},{3,4},{4,5},{5,6},{6,7},{7,0},{8,9},{9,10},{10,1... | collective-permute-start | bytes 1658888 | tf_op jit(solution)/shard_map/ppermute | solution.py:428
  349.7 3.6 copy-start.1
  350.7 21.2 %collective-permute-start.15 = (bf16[9,3,80,128]{3,2,1,0:T(8,128)(2,1)}, bf16[9,3,80,128]{3,2,1,0:T(8,128)(2,1)S(1)}, u32[]{:S(2)}, u32[]{:S(2)}) collective-permute-start(bf16[9,3,80,128]{3,2,1,0:T(8,128)(2,1)} %slice.19), channel_id=1, source_target_pairs={{0,7},{1,0},{2,1},{3,2},{4,3},{5,4},{6,5},{7,6},{8,15},{9,8},{10,9... | collective-permute-start | bytes 1658888 | tf_op jit(solution)/shard_map/ppermute | solution.py:429
  371.9 0.8 copy-start.4
  371.9 1.0 copy-start.5

commit v2 on v1

--- a/solution.py
+++ b/solution.py
@@ -80,39 +80,41 @@
         u, r, s = unit(q), turn(q), lax.rem(q, SLOTS)
         ca, cb = (pl.ds(0, lanes),) * 2 if both else (pl.ds(0, half), pl.ds(half, half))
         return (
-            pltpu.make_async_remote_copy(
+            lambda: pltpu.make_async_remote_copy(
                 g_ref.at[u, ca, shard(me + rounds - r)], ra.at[s, ca], sem_sa.at[s], sem_ra.at[s],
                 device_id={"dp": right}, device_id_type=MESH,
             ),
-            pltpu.make_async_remote_copy(
+            lambda: pltpu.make_async_remote_copy(
                 g_ref.at[u, cb, shard(me + n - rounds + r)], rb.at[s, cb], sem_sb.at[s], sem_rb.at[s],
                 device_id={"dp": left}, device_id_type=MESH,
             ),
         )
 
-    def each(q, what):
+    def each(q, what, sides=(0, 1)):
         r = turn(q)
 
         @pl.when(r == 0)
         def _():
-            for copy in copies(q, False):
-                what(copy)
+            for side in sides:
+                what(copies(q, False)[side]())
 
         @pl.when(r > 0)
         def _():
-            for copy in copies(q, True):
-                what(copy)
-
-    def send(q):
+            for side in sides:
+                what(copies(q, True)[side]())
+
+    free = free_a, free_b
+
+    def send(q, sides=(0, 1)):
         @pl.when(valid(q))
         def _():
             @pl.when(valid(q - SLOTS))
             def _():
-                pl.semaphore_wait(free_a.at[lax.rem(q, SLOTS)], 1)
-                pl.semaphore_wait(free_b.at[lax.rem(q, SLOTS)], 1)
-                each(q - SLOTS, lambda c: c.wait_send())
-
-            each(q, lambda c: c.start())
+                for side in sides:
+                    pl.semaphore_wait(free[side].at[lax.rem(q, SLOTS)], 1)
+                each(q - SLOTS, lambda c: c.wait_send(), sides)
+
+            each(q, lambda c: c.start(), sides)
 
     def own(u, what):
         def to(out, k):
@@ -138,34 +140,38 @@
         def _():
             u, r, s = unit(q), turn(q), lax.rem(q, SLOTS)
             at, bt = shard(me + rounds - 1 - r), shard(me + n - rounds + 1 + r)
-            each(q, lambda c: c.wait_recv())
-
-            @pl.when(r == 0)
-            def _():
-                g_ref[u, :half, at] = (wide(g_ref[u, :half, at]) + wide(ra[s, :half])).astype(bf16)
-                g_ref[u, half:, bt] = (wide(g_ref[u, half:, bt]) + wide(rb[s, half:])).astype(bf16)
-
-            @pl.when(jnp.logical_and(r > 0, r < rounds - 1))
-            def _():
-                g_ref[u, :, at] = (wide(g_ref[u, :, at]) + wide(ra[s])).astype(bf16)
-                g_ref[u, :, bt] = (wide(g_ref[u, :, bt]) + wide(rb[s])).astype(bf16)
+
+            def done_with(side):
+                @pl.when(valid(q + SLOTS))
+                def _():
+                    to = (left, right)[side]
+                    pl.semaphore_signal(free[side].at[s], inc=1, device_id={"dp": to}, device_id_type=MESH)
+
+            for side, (got, where, lo, hi) in enumerate(((ra, at, 0, half), (rb, bt, half, lanes))):
+                each(q, lambda c: c.wait_recv(), (side,))
+
+                @pl.when(r == 0)
+                def _(got=got, where=where, lo=lo, hi=hi):
+                    g_ref[u, lo:hi, where] = (wide(g_ref[u, lo:hi, where]) + wide(got[s, lo:hi])).astype(bf16)
+
+                @pl.when(jnp.logical_and(r > 0, r < rounds - 1))
+                def _(got=got, where=where):
+                    g_ref[u, :, where] = (wide(g_ref[u, :, where]) + wide(got[s])).astype(bf16)
+
+                @pl.when(r < rounds - 1)
+                def _(side=side):
+                    send(q + STAGGER * rounds - 1, (side,))
+                    done_with(side)
 
             @pl.when(r == rounds - 1)
             def _():
                 g_ref[u, :, at] = (wide(g_ref[u, :, at]) + wide(ra[s]) + wide(rb[s])).astype(bf16)
-
-            @pl.when(valid(q + SLOTS))
-            def _():
-                pl.semaphore_signal(free_a.at[s], inc=1, device_id={"dp": left}, device_id_type=MESH)
-                pl.semaphore_signal(free_b.at[s], inc=1, device_id={"dp": right}, device_id_type=MESH)
+                done_with(0)
+                done_with(1)
 
             @pl.when(r == rounds - 1)
             def _():
                 own(u, lambda c: c.start())
-
-            @pl.when(r < rounds - 1)
-            def _():
-                send(q + STAGGER * rounds - 1)
 
             @pl.when(jnp.logical_and(r == 0, u + LEAD < ready))
             def _():

time: 392 us -> 394 us (level)
  no operation moved by 1% of the time
where the time goes in v2:
time: 394 us; the launch traced here: 388 us
  Pallas kernels  293 us (74%)
  waiting for transfers between devices  66.2 us (17%)
  starting transfers between devices  19.4 us (5%)
  local copies, waits for them, and re-layouts  5.76 us (1%)
    pallas_call x1, Pallas kernels, train(): pl.pallas_call(functools.partial(train_kernel, n), out_shape=tuple((jax.S...  213 us
    pallas_call x10, Pallas kernels, optimizer(): pl.pallas_call(functools.partial(adamw_kernel, len(shards), paired, 1 - l...  80.9 us
    ppermute x8, waiting for transfers between devices, both(): from_left = lax.ppermute(to_right, 'dp', right)  45.3 us
    ppermute x8, waiting for transfers between devices, both(): return (from_left, lax.ppermute(to_left, 'dp', left))  20.8 us
    ppermute x8, starting transfers between devices, both(): return (from_left, lax.ppermute(to_left, 'dp', left))  18.9 us
  transfers between devices with their start and end apart: 16, of which 5 were waited for; matrix products, arithmetic and copies ran while one was open for 2% of the time, Pallas kernels for 19%

profile of v2, /device:TPU:21, one launch (start us, length us, event | category | flops | bytes accessed | tf_op | source)
XLA Modules:
  0.0 387.5 jit_solution(547079373861278375)
XLA Ops:
  0.6 212.5 %train.1 = (bf16[9,6,80,128]{3,2,1,0:T(8,128)(2,1)}, bf16[8,6,80,128]{3,2,1,0:T(8,128)(2,1)}) custom-call(bf16[2048,640]{1,0:T(8,128)(2,1)} %bitcast.42, bf16[2048,640]{1,0:T(8,128)(2,1)} %bitcast.43, bf16[2,640,2176]{2,1,0:T(8,128)(2,1)} %refs_4_.11, bf16[2,640,2176]{2,1,0:T(8,128)(2,1)} %refs_5_.19, bf16[2,2176,640]{2,1,0:T(8,128)(2,1)} %refs_4_.6), custom_call_target="tpu_custom_call" | custom-call | flops 85563801600 | bytes 55705600 | tf_op jit(solution)/shard_map/train/pallas_call | solution.py:411
  213.2 1.2 collective-permute-start.12
  214.3 0.4 collective-permute-start.8
  214.7 0.0 collective-permute-start
  214.8 2.7 collective-permute-start.4
  217.4 20.8 %collective-permute-done.12.refs_1_.refs_3_ = bf16[9,6,80,128]{3,2,1,0:T(8,128)(2,1)S(1)} collective-permute-done((bf16[9,6,80,128]{3,2,1,0:T(8,128)(2,1)}, bf16[9,6,80,128]{3,2,1,0:T(8,128)(2,1)S(1)}, u32[]{:S(2)}, u32[]{:S(2)}) %collective-permute-start.12) | collective-permute-done | bytes 1105952 | tf_op jit(solution)/shard_map/ppermute | solution.py:435
  238.2 0.0 copy-start.2
  238.2 1.8 collective-permute-start.13
  240.0 0.0 collective-permute-done.8.refs_0_.refs_2_
  240.0 0.0 copy-start.3
  240.0 0.0 collective-permute-start.9
  240.1 0.7 pad_add_fusion.2.ids_ref
  240.8 20.1 %collective-permute-done.refs_0_ = bf16[8,6,80,128]{3,2,1,0:T(8,128)(2,1)} collective-permute-done((bf16[8,6,80,128]{3,2,1,0:T(8,128)(2,1)}, bf16[8,6,80,128]{3,2,1,0:T(8,128)(2,1)}, u32[]{:S(2)}, u32[]{:S(2)}) %collective-permute-start) | collective-permute-done | bytes 983072 | tf_op jit(solution)/shard_map/ppermute | solution.py:434
  260.9 0.0 collective-permute-start.1
  260.9 0.0 collective-permute-done.4.refs_1_
  260.9 2.7 collective-permute-start.5
  263.6 0.6 pad_add_fusion.1.ids_ref
  264.2 0.7 pad_add_fusion.ids_ref
  264.9 6.4 %adamw.10 = (bf16[2,640,2176]{2,1,0:T(8,128)(2,1)}, bf16[2,640,2176]{2,1,0:T(8,128)(2,1)}, bf16[2,17,128,640]{3,2,1,0:T(8,128)(2,1)}, f32[2,640,2176]{2,1,0:T(8,...) custom-call(s32[1]{0:T(128)S(6)} %rem.159.ids_ref, ...), custom_call_target="tpu_custom_call" | custom-call | flops 2088960000 | bytes 11489280 | tf_op jit(solution)/shard_map/adamw/pallas_call | solution.py:505
  271.2 0.0 copy-done.2
  271.2 0.0 copy-done.3
  271.2 6.5 %adamw.11 = (bf16[2,640,2176]{2,1,0:T(8,128)(2,1)}, bf16[2,640,2176]{2,1,0:T(8,128)(2,1)}, bf16[2,17,128,640]{3,2,1,0:T(8,128)(2,1)}, f32[2,640,2176]{2,1,0:T(8,...) custom-call(s32[1]{0:T(128)S(6)} %rem.159.ids_ref, ...), custom_call_target="tpu_custom_call", output_to_operand_aliasing={{0}: (12, {}), {1}: (13, {}), {2}: (14, {}), {3}: (15, {}),... | custom-call | flops 2088960000 | bytes 11489280 | tf_op jit(solution)/shard_map/adamw/pallas_call | solution.py:505
  277.7 9.2 %adamw.12 = (bf16[2,640,2176]{2,1,0:T(8,128)(2,1)}, bf16[2,640,2176]{2,1,0:T(8,128)(2,1)}, bf16[2,17,128,640]{3,2,1,0:T(8,128)(2,1)}, f32[2,640,2176]{2,1,0:T(8,...) custom-call(s32[2]{0:T(128)} %pad_add_fusion.2.ids_ref, ...), custom_call_target="tpu_custom_call", output_to_operand_aliasing={{0}: (12, {}), {1}: (13, {}), {2}: (14, {}), {3}: (15, {}),... | custom-call | flops 4177920000 | bytes 22978560 | tf_op jit(solution)/shard_map/adamw/pallas_call | solution.py:505
  286.9 18.8 %collective-permute-done.1.refs_0_ = bf16[8,6,80,128]{3,2,1,0:T(8,128)(2,1)} collective-permute-done((bf16[8,6,80,128]{3,2,1,0:T(8,128)(2,1)}, bf16[8,6,80,128]{3,2,1,0:T(8,128)(2,1)}, u32[]{:S(2)}, u32[]{:S(2)}) %collective-permute-start.1) | collective-permute-done | bytes 983072 | tf_op jit(solution)/shard_map/ppermute | solution.py:434
  305.7 0.0 collective-permute-start.2
  305.7 0.0 collective-permute-done.5.refs_1_
  305.7 0.0 copy-start.6
  305.7 2.7 collective-permute-start.6
  308.4 0.0 collective-permute-done.9.refs_0_.refs_2_
  308.4 0.0 collective-permute-start.10
  308.4 0.0 collective-permute-done.13.refs_1_.refs_3_
  308.4 2.7 collective-permute-start.14
  311.1 9.1 %adamw.13 = (bf16[2,640,2176]{2,1,0:T(8,128)(2,1)}, bf16[2,640,2176]{2,1,0:T(8,128)(2,1)}, bf16[2,17,128,640]{3,2,1,0:T(8,128)(2,1)}, f32[2,640,2176]{2,1,0:T(8,...) custom-call(s32[2]{0:T(128)} %pad_add_fusion.2.ids_ref, ...), custom_call_target="tpu_custom_call", output_to_operand_aliasing={{0}: (14, {}), {1}: (15, {}), {2}: (16, {}), {3}: (17, {}),... | custom-call | flops 4177920000 | bytes 22978560 | tf_op jit(solution)/shard_map/adamw/pallas_call | solution.py:505
  320.2 0.0 copy-done.6
  320.2 9.3 %adamw.14 = (bf16[2,640,2176]{2,1,0:T(8,128)(2,1)}, bf16[2,640,2176]{2,1,0:T(8,128)(2,1)}, bf16[2,17,128,640]{3,2,1,0:T(8,128)(2,1)}, f32[2,640,2176]{2,1,0:T(8,...) custom-call(s32[2]{0:T(128)} %pad_add_fusion.1.ids_ref, ...), custom_call_target="tpu_custom_call", output_to_operand_aliasing={{0}: (12, {}), {1}: (13, {}), {2}: (14, {}), {3}: (15, {}),... | custom-call | flops 4177920000 | bytes 22978560 | tf_op jit(solution)/shard_map/adamw/pallas_call | solution.py:505
  329.5 9.2 %adamw.15 = (bf16[2,640,2176]{2,1,0:T(8,128)(2,1)}, bf16[2,640,2176]{2,1,0:T(8,128)(2,1)}, bf16[2,17,128,640]{3,2,1,0:T(8,128)(2,1)}, f32[2,640,2176]{2,1,0:T(8,...) custom-call(s32[2]{0:T(128)} %pad_add_fusion.1.ids_ref, ...), custom_call_target="tpu_custom_call", output_to_operand_aliasing={{0}: (14, {}), {1}: (15, {}), {2}: (16, {}), {3}: (17, {}),... | custom-call | flops 4177920000 | bytes 22978560 | tf_op jit(solution)/shard_map/adamw/pallas_call | solution.py:505
  338.7 0.0 collective-permute-done.2.refs_0_
  338.7 1.8 slice.16
  340.6 0.0 collective-permute-start.3
  340.6 0.0 collective-permute-done.6.refs_1_
  340.6 1.8 slice.17
  342.4 2.7 collective-permute-start.7
  345.1 6.2 %collective-permute-done.10.refs_0_.refs_2_ = bf16[9,6,80,128]{3,2,1,0:T(8,128)(2,1)S(1)} collective-permute-done((bf16[9,6,80,128]{3,2,1,0:T(8,128)(2,1)}, bf16[9,6,80,128]{3,2,1,0:T(8,128)(2,1)S(1)}, u32[]{:S(2)}, u32[]{:S(2)}) %collective-permute-start.10) | collective-permute-done | bytes 1105952 | tf_op jit(solution)/shard_map/ppermute | solution.py:434
  351.3 0.0 copy-start
  351.4 0.1 collective-permute-start.11
  351.5 0.0 collective-permute-done.14.refs_1_.refs_3_
  351.5 0.0 copy-start.1
  351.5 1.0 slice.19
  352.5 2.5 collective-permute-start.15
  355.1 0.0 copy-done
  355.1 0.0 copy-done.1
  355.1 9.2 %adamw.16 = (bf16[2,640,2176]{2,1,0:T(8,128)(2,1)}, bf16[2,640,2176]{2,1,0:T(8,128)(2,1)}, bf16[2,17,128,640]{3,2,1,0:T(8,128)(2,1)}, f32[2,640,2176]{2,1,0:T(8,...) custom-call(s32[2]{0:T(128)} %pad_add_fusion.ids_ref, ...), custom_call_target="tpu_custom_call", output_to_operand_aliasing={{0}: (12, {}), {1}: (13, {}), {2}: (14, {}), {3}: (15, {}),... | custom-call | flops 4177920000 | bytes 22978560 | tf_op jit(solution)/shard_map/adamw/pallas_call | solution.py:505
  364.3 9.2 %adamw.17 = (bf16[2,640,2176]{2,1,0:T(8,128)(2,1)}, bf16[2,640,2176]{2,1,0:T(8,128)(2,1)}, bf16[2,17,128,640]{3,2,1,0:T(8,128)(2,1)}, f32[2,640,2176]{2,1,0:T(8,...) custom-call(s32[2]{0:T(128)} %pad_add_fusion.ids_ref, ...), custom_call_target="tpu_custom_call", output_to_operand_aliasing={{0}: (14, {}), {1}: (15, {}), {2}: (16, {}), {3}: (17, {}),... | custom-call | flops 4177920000 | bytes 22978560 | tf_op jit(solution)/shard_map/adamw/pallas_call | solution.py:505
  373.5 0.2 collective-permute-done.11.refs_0_.refs_2_
  373.7 0.0 copy-start.4
  373.7 0.0 collective-permute-done.15.refs_1_.refs_3_
  373.7 0.0 copy-start.5
  373.7 0.8 copy-done.4
  374.5 0.2 copy-done.5
  374.7 6.4 %adamw.18 = (bf16[2,640,2176]{2,1,0:T(8,128)(2,1)}, bf16[2,640,2176]{2,1,0:T(8,128)(2,1)}, bf16[2,17,128,640]{3,2,1,0:T(8,128)(2,1)}, f32[2,640,2176]{2,1,0:T(8,...) custom-call(s32[1]{0:T(128)S(6)} %rem.117.ids_ref, ...), custom_call_target="tpu_custom_call", output_to_operand_aliasing={{0}: (12, {}), {1}: (13, {}), {2}: (14, {}), {3}: (15, {}),... | custom-call | flops 2088960000 | bytes 11489280 | tf_op jit(solution)/shard_map/adamw/pallas_call | solution.py:505
  381.1 0.0 collective-permute-done.3.refs_0_
  381.1 0.0 collective-permute-done.7.refs_1_
  381.1 6.4 %adamw.19 = (bf16[2,640,2176]{2,1,0:T(8,128)(2,1)}, bf16[2,640,2176]{2,1,0:T(8,128)(2,1)}, bf16[2,17,128,640]{3,2,1,0:T(8,128)(2,1)}, f32[2,640,2176]{2,1,0:T(8,...) custom-call(s32[1]{0:T(128)S(6)} %rem.117.ids_ref, ...), custom_call_target="tpu_custom_call", output_to_operand_aliasing={{0}: (14, {}), {1}: (15, {}), {2}: (16, {}), {3}: (17, {}),... | custom-call | flops 2088960000 | bytes 11489280 | tf_op jit(solution)/shard_map/adamw/pallas_call | solution.py:505
  (1 shorter events, 0.0 us)
Async XLA Ops:
  213.2 25.0 %collective-permute-start.12 = (bf16[9,6,80,128]{3,2,1,0:T(8,128)(2,1)}, bf16[9,6,80,128]{3,2,1,0:T(8,128)(2,1)S(1)}, u32[]{:S(2)}, u32[]{:S(2)}) collective-permute-start(bf16[9,6,80,128]{3,2,1,0:T(8,128)(2,1)} %get-tuple-element.102.refs_0_.refs_1_), channel_id=1, source_target_pairs={{0,7},{1,0},{2,1},{3,2},{4,3},{5,4},{6,5},{7,6},{8,15},{9,8},{10,9... | collective-permute-start | bytes 3317768 | tf_op jit(solution)/shard_map/ppermute | solution.py:435
  214.3 25.7 %collective-permute-start.8 = (bf16[9,6,80,128]{3,2,1,0:T(8,128)(2,1)}, bf16[9,6,80,128]{3,2,1,0:T(8,128)(2,1)S(1)}, u32[]{:S(2)}, u32[]{:S(2)}) collective-permute-start(bf16[9,6,80,128]{3,2,1,0:T(8,128)(2,1)} %get-tuple-element.102.refs_0_.refs_1_), channel_id=1, source_target_pairs={{0,1},{1,2},{2,3},{3,4},{4,5},{5,6},{6,7},{7,0},{8,9},{9,10},{10,1... | collective-permute-start | bytes 3317768 | tf_op jit(solution)/shard_map/ppermute | solution.py:434
  214.7 46.2 %collective-permute-start = (bf16[8,6,80,128]{3,2,1,0:T(8,128)(2,1)}, bf16[8,6,80,128]{3,2,1,0:T(8,128)(2,1)}, u32[]{:S(2)}, u32[]{:S(2)}) collective-permute-start(bf16[8,6,80,128]{3,2,1,0:T(8,128)(2,1)} %get-tuple-element.101.refs_0_), channel_id=1, source_target_pairs={{0,1},{1,2},{2,3},{3,4},{4,5},{5,6},{6,7},{7,0},{8,9},{9,10},{10,1... | collective-permute-start | bytes 2949128 | tf_op jit(solution)/shard_map/ppermute | solution.py:434
  214.8 46.2 %collective-permute-start.4 = (bf16[8,6,80,128]{3,2,1,0:T(8,128)(2,1)}, bf16[8,6,80,128]{3,2,1,0:T(8,128)(2,1)}, u32[]{:S(2)}, u32[]{:S(2)}) collective-permute-start(bf16[8,6,80,128]{3,2,1,0:T(8,128)(2,1)} %get-tuple-element.101.refs_0_), channel_id=1, source_target_pairs={{0,7},{1,0},{2,1},{3,2},{4,3},{5,4},{6,5},{7,6},{8,15},{9,8},{10,9... | collective-permute-start | bytes 2949128 | tf_op jit(solution)/shard_map/ppermute | solution.py:435
  238.2 33.0 %copy-start.2 = (bf16[9,6,80,128]{3,2,1,0:T(8,128)(2,1)}, bf16[9,6,80,128]{3,2,1,0:T(8,128)(2,1)S(1)}, u32[]{:S(2)}) copy-start(bf16[9,6,80,128]{3,2,1,0:T(8,128)(2,1)S(1)} %collective-permute-done.12.refs_1_.refs_3_) | copy-start | bytes 3317764
  238.2 70.2 %collective-permute-start.13 = (bf16[9,6,80,128]{3,2,1,0:T(8,128)(2,1)S(1)}, bf16[9,6,80,128]{3,2,1,0:T(8,128)(2,1)}, u32[]{:S(2)}, u32[]{:S(2)}) collective-permute-start(bf16[9,6,80,128]{3,2,1,0:T(8,128)(2,1)S(1)} %collective-permute-done.12.refs_1_.refs_3_), channel_id=1, source_target_pairs={{0,7},{1,0},{2,1},{3,2},{4,3},{5,4},{6,5},{7,6},{8,15},{9,8},{10,9... | collective-permute-start | bytes 3317768 | tf_op jit(solution)/shard_map/ppermute | solution.py:435
  240.0 31.2 %copy-start.3 = (bf16[9,6,80,128]{3,2,1,0:T(8,128)(2,1)}, bf16[9,6,80,128]{3,2,1,0:T(8,128)(2,1)S(1)}, u32[]{:S(2)}) copy-start(bf16[9,6,80,128]{3,2,1,0:T(8,128)(2,1)S(1)} %collective-permute-done.8.refs_0_.refs_2_) | copy-start | bytes 3317764
  240.0 68.3 %collective-permute-start.9 = (bf16[9,6,80,128]{3,2,1,0:T(8,128)(2,1)S(1)}, bf16[9,6,80,128]{3,2,1,0:T(8,128)(2,1)}, u32[]{:S(2)}, u32[]{:S(2)}) collective-permute-start(bf16[9,6,80,128]{3,2,1,0:T(8,128)(2,1)S(1)} %collective-permute-done.8.refs_0_.refs_2_), channel_id=1, source_target_pairs={{0,1},{1,2},{2,3},{3,4},{4,5},{5,6},{6,7},{7,0},{8,9},{9,10},{10,1... | collective-permute-start | bytes 3317768 | tf_op jit(solution)/shard_map/ppermute | solution.py:434
  260.9 44.8 %collective-permute-start.1 = (bf16[8,6,80,128]{3,2,1,0:T(8,128)(2,1)}, bf16[8,6,80,128]{3,2,1,0:T(8,128)(2,1)}, u32[]{:S(2)}, u32[]{:S(2)}) collective-permute-start(bf16[8,6,80,128]{3,2,1,0:T(8,128)(2,1)} %collective-permute-done.refs_0_), channel_id=1, source_target_pairs={{0,1},{1,2},{2,3},{3,4},{4,5},{5,6},{6,7},{7,0},{8,9},{9,10},{10,1... | collective-permute-start | bytes 2949128 | tf_op jit(solution)/shard_map/ppermute | solution.py:434
  260.9 44.8 %collective-permute-start.5 = (bf16[8,6,80,128]{3,2,1,0:T(8,128)(2,1)}, bf16[8,6,80,128]{3,2,1,0:T(8,128)(2,1)S(1)}, u32[]{:S(2)}, u32[]{:S(2)}) collective-permute-start(bf16[8,6,80,128]{3,2,1,0:T(8,128)(2,1)} %collective-permute-done.4.refs_1_), channel_id=1, source_target_pairs={{0,7},{1,0},{2,1},{3,2},{4,3},{5,4},{6,5},{7,6},{8,15},{9,8},{10,9... | collective-permute-start | bytes 2949128 | tf_op jit(solution)/shard_map/ppermute | solution.py:435
  305.7 33.0 %collective-permute-start.2 = (bf16[8,6,80,128]{3,2,1,0:T(8,128)(2,1)}, bf16[8,6,80,128]{3,2,1,0:T(8,128)(2,1)}, u32[]{:S(2)}, u32[]{:S(2)}) collective-permute-start(bf16[8,6,80,128]{3,2,1,0:T(8,128)(2,1)} %collective-permute-done.1.refs_0_), channel_id=1, source_target_pairs={{0,1},{1,2},{2,3},{3,4},{4,5},{5,6},{6,7},{7,0},{8,9},{9,10},{10,1... | collective-permute-start | bytes 2949128 | tf_op jit(solution)/shard_map/ppermute | solution.py:434
  305.7 14.5 %copy-start.6 = (bf16[8,6,80,128]{3,2,1,0:T(8,128)(2,1)}, bf16[8,6,80,128]{3,2,1,0:T(8,128)(2,1)S(1)}, u32[]{:S(2)}) copy-start(bf16[8,6,80,128]{3,2,1,0:T(8,128)(2,1)S(1)} %collective-permute-done.5.refs_1_) | copy-start | bytes 2949124
  305.7 34.9 %collective-permute-start.6 = (bf16[8,6,80,128]{3,2,1,0:T(8,128)(2,1)S(1)}, bf16[8,6,80,128]{3,2,1,0:T(8,128)(2,1)}, u32[]{:S(2)}, u32[]{:S(2)}) collective-permute-start(bf16[8,6,80,128]{3,2,1,0:T(8,128)(2,1)S(1)} %collective-permute-done.5.refs_1_), channel_id=1, source_target_pairs={{0,7},{1,0},{2,1},{3,2},{4,3},{5,4},{6,5},{7,6},{8,15},{9,8},{10,9... | collective-permute-start | bytes 2949128 | tf_op jit(solution)/shard_map/ppermute | solution.py:435
  308.4 42.9 %collective-permute-start.10 = (bf16[9,6,80,128]{3,2,1,0:T(8,128)(2,1)}, bf16[9,6,80,128]{3,2,1,0:T(8,128)(2,1)S(1)}, u32[]{:S(2)}, u32[]{:S(2)}) collective-permute-start(bf16[9,6,80,128]{3,2,1,0:T(8,128)(2,1)} %collective-permute-done.9.refs_0_.refs_2_), channel_id=1, source_target_pairs={{0,1},{1,2},{2,3},{3,4},{4,5},{5,6},{6,7},{7,0},{8,9},{9,10},{10,1... | collective-permute-start | bytes 3317768 | tf_op jit(solution)/shard_map/ppermute | solution.py:434
  308.4 43.1 %collective-permute-start.14 = (bf16[9,6,80,128]{3,2,1,0:T(8,128)(2,1)}, bf16[9,6,80,128]{3,2,1,0:T(8,128)(2,1)S(1)}, u32[]{:S(2)}, u32[]{:S(2)}) collective-permute-start(bf16[9,6,80,128]{3,2,1,0:T(8,128)(2,1)} %collective-permute-done.13.refs_1_.refs_3_), channel_id=1, source_target_pairs={{0,7},{1,0},{2,1},{3,2},{4,3},{5,4},{6,5},{7,6},{8,15},{9,8},{10,9... | collective-permute-start | bytes 3317768 | tf_op jit(solution)/shard_map/ppermute | solution.py:435
  340.6 40.5 %collective-permute-start.3 = (bf16[8,3,80,128]{3,2,1,0:T(8,128)(2,1)}, bf16[8,3,80,128]{3,2,1,0:T(8,128)(2,1)}, u32[]{:S(2)}, u32[]{:S(2)}) collective-permute-start(bf16[8,3,80,128]{3,2,1,0:T(8,128)(2,1)} %slice.16), channel_id=1, source_target_pairs={{0,1},{1,2},{2,3},{3,4},{4,5},{5,6},{6,7},{7,0},{8,9},{9,10},{10,1... | collective-permute-start | bytes 1474568 | tf_op jit(solution)/shard_map/ppermute | solution.py:434
  342.4 38.6 %collective-permute-start.7 = (bf16[8,3,80,128]{3,2,1,0:T(8,128)(2,1)}, bf16[8,3,80,128]{3,2,1,0:T(8,128)(2,1)}, u32[]{:S(2)}, u32[]{:S(2)}) collective-permute-start(bf16[8,3,80,128]{3,2,1,0:T(8,128)(2,1)} %slice.17), channel_id=1, source_target_pairs={{0,7},{1,0},{2,1},{3,2},{4,3},{5,4},{6,5},{7,6},{8,15},{9,8},{10,9... | collective-permute-start | bytes 1474568 | tf_op jit(solution)/shard_map/ppermute | solution.py:435
  351.3 3.7 copy-start
  351.4 22.3 %collective-permute-start.11 = (bf16[9,3,80,128]{3,2,1,0:T(8,128)(2,1)S(1)}, bf16[9,3,80,128]{3,2,1,0:T(8,128)(2,1)S(1)}, u32[]{:S(2)}, u32[]{:S(2)}) collective-permute-start(bf16[9,3,80,128]{3,2,1,0:T(8,128)(2,1)S(1)} %slice.18), channel_id=1, source_target_pairs={{0,1},{1,2},{2,3},{3,4},{4,5},{5,6},{6,7},{7,0},{8,9},{9,10},{10,1... | collective-permute-start | bytes 1658888 | tf_op jit(solution)/shard_map/ppermute | solution.py:434
  351.5 3.6 copy-start.1
  352.5 21.2 %collective-permute-start.15 = (bf16[9,3,80,128]{3,2,1,0:T(8,128)(2,1)}, bf16[9,3,80,128]{3,2,1,0:T(8,128)(2,1)S(1)}, u32[]{:S(2)}, u32[]{:S(2)}) collective-permute-start(bf16[9,3,80,128]{3,2,1,0:T(8,128)(2,1)} %slice.19), channel_id=1, source_target_pairs={{0,7},{1,0},{2,1},{3,2},{4,3},{5,4},{6,5},{7,6},{8,15},{9,8},{10,9... | collective-permute-start | bytes 1658888 | tf_op jit(solution)/shard_map/ppermute | solution.py:435
  373.7 0.8 copy-start.4
  373.7 1.0 copy-start.5
